TPU v7x, 256 devices: a 4x2x16 block of a 4x16x16 slice. The times are simulated.
256 devices in a mesh: groups: 2 (over y), seq: 16 (over z), head: 8 (over x, core).
Axes of the slice: x: 4, y: 2, z: 16, core: 2. Of those that a mesh axis runs over, the one named last changes fastest.
The devices are a block of a 4x16x16 slice.
Arguments:
- residual: bfloat16 [16384, 2560], P(('groups', 'seq'), 'head'), parts along dimension 0, may hold values from -6 to 6
- x_in: bfloat16 [16384, 5120], P(('groups', 'seq'), 'head'), parts along dimension 0, may hold values from -6 to 6
- bc_in: bfloat16 [16384, 256], P(('groups', 'seq')), parts along dimension 0, may hold values from -1.5 to 1.5
- z_in: bfloat16 [16384, 5120], P(('groups', 'seq'), 'head'), parts along dimension 0, may hold values from -6 to 6
- dt_raw: float32 [80, 16384], P('head', ('groups', 'seq')), parts along dimension 1, may hold values from -5 to 5
- dt_bias: float32 [80], P('head'), may hold values from -3 to 0
- decay_rate: float32 [80], P('head'), may hold values from 0.0003 to 0.15
- d_skip: float32 [80], P('head'), may hold values from 1 to 4
- conv_x_weight: bfloat16 [4, 5120], P(None, 'head'), may hold values from -3 to 3
- conv_x_bias: bfloat16 [5120], P('head'), may hold values from -3 to 3
- conv_bc_weight: bfloat16 [4, 256], replicated, may hold values from -3 to 3
- conv_bc_bias: bfloat16 [256], replicated, may hold values from -3 to 3
- norm_gain: bfloat16 [5120], P('head'), may hold values from 0.5 to 1.5
- out_weight: bfloat16 [5120, 2560], P('head'), may hold values from -0.078125 to 0.078125
- final_gain: bfloat16 [2560], replicated, may hold values from 0.5 to 1.5
- lm_weight: bfloat16 [2560, 25600], P('seq', 'head'), may hold values from -15.811388 to 15.811388
- targets: int32 [16384], P(('groups', 'seq')), parts along dimension 0, may hold values from 0 to 25599
- doc_lengths: int32 [32], P('groups'), parts along dimension 0, may hold values from 1 to 1536, as said below
Outputs:
- block_out: bfloat16 [16384, 2560], P(('groups', 'seq'), 'head'), parts along dimension 0
- doc_loss: float32 [32], P('groups'), parts along dimension 0
There are 2 independent parts, one for each index of `groups`. A program takes and returns all parts, laid end to end along the dimension named above; an argument that names none is the same for every part. Nothing has to cross between parts.
Inputs may be any that keep to these rules, and one draw needn't show every extreme that they name: `doc_lengths`: the lengths of a group's 16 documents, in the order in which they are packed into its 8192 tokens; they sum to 8192.
All inputs are finite; a program needn't handle non-finite values.
Results may differ from a plain program's by a relative error of at most 0.00145.
The roundings to bfloat16 on the way count: a program that leaves them out, or rounds other values in their place, can miss the bound.
Values may be sent and summed in bfloat16 or wider, within the bound.
No kernel may reach another device: no remote copies, remote signals or barrier semaphores. Data moves between devices by JAX's collectives and lax.ppermute only.
A program may use at most 128 MiB of HBM per device.

v0:
```python
import jax
import jax.numpy as jnp
from jax import lax
from jax.sharding import PartitionSpec as P

D = 2560
HEAD_SIZE = 64
STATE = 128
KERNEL = 4
SPAN = 256
INNER = 5120


EPSILON = 1e-05
HIGH = lax.Precision.HIGHEST


def shifted(array, axis, by):
    length = lax.axis_size(axis)
    pairs = [(i, i + by) for i in range(length) if 0 <= i + by < length]
    return lax.ppermute(array, axis, pairs)


def entering(part, axis, combine, identity):
    place = lax.axis_index(axis)
    gathered = jax.tree.map(lambda a: lax.all_gather(a, axis), part)
    state = jax.tree.map(lambda a, e: jnp.zeros_like(a) + jnp.asarray(e, a.dtype), part, identity)

    def one(lap, state):
        return combine(
            state, jax.tree.map(lambda a: lax.dynamic_index_in_dim(a, lap, 0, False), gathered)
        )

    return lax.fori_loop(0, place, one, state)


def cut_along(array, dim, length):
    shape = array.shape
    blocks = array.reshape(*shape[:dim], length, shape[dim] // length, *shape[dim + 1 :])
    return jnp.moveaxis(blocks, dim, 0)


def sent_and_summed(array, axis, dim):
    blocks = cut_along(array, dim, lax.axis_size(axis))
    arrived = lax.all_to_all(blocks, axis, split_axis=0, concat_axis=0, tiled=True)
    return arrived.sum(axis=0)


def joined_along(blocks, dim):
    shape = list(blocks.shape[1:])
    shape[dim] *= blocks.shape[0]
    return jnp.moveaxis(blocks, 0, dim).reshape(shape)


def from_everyone(array, axis):
    length = lax.axis_size(axis)
    return lax.all_to_all(
        jnp.broadcast_to(array[None], (length, *array.shape)), axis, 0, 0, tiled=True
    )


def gather_directly(array, axis, dim):
    return joined_along(from_everyone(array, axis), dim)


def gathered_once(array, axis):
    leaves = jax.tree.leaves(array)
    sequence = sorted(range(len(leaves)), key=lambda k: -leaves[k].size)
    width = (1, *leaves[sequence[0]].shape)[-1]
    lines = [
        jnp.pad(leaves[k].reshape(-1), (0, -leaves[k].size % width)).reshape(-1, width)
        for k in sequence
    ]
    both, at, found = (lax.all_gather(jnp.concatenate(lines), axis), 0, {})
    for k, line in zip(sequence, lines):
        section = both[:, at : at + len(line)].reshape(len(both), -1)
        found[k] = section[:, : leaves[k].size].reshape(-1, *leaves[k].shape)
        at += len(line)
    numbers = iter(range(len(leaves)))
    return jax.tree.map(lambda _: found[next(numbers)], array)


def joined_2(part, axis, combine):
    gathered = gathered_once(part, axis)

    def take(source):
        return jax.tree.map(lambda a: lax.dynamic_index_in_dim(a, source, 0, False), gathered)

    return lax.fori_loop(
        1, lax.axis_size(axis), lambda source, state: combine(state, take(source)), take(0)
    )


def over_copies(array, axis):
    return from_everyone(array, axis).sum(axis=0)


def document_of(positions, doc_lengths):
    starts = jnp.cumsum(doc_lengths) - doc_lengths
    return jnp.sum((positions[:, None] >= starts[None, :]).astype(jnp.int32), axis=1) - 1


def causal_conv(signal, rim_rows, weight, bias, positions, doc_ids, doc_lengths):
    length = signal.shape[0]
    taps = weight.shape[0]
    joined = jnp.concatenate([rim_rows, signal], axis=0).astype(jnp.float32)
    total = jnp.zeros(signal.shape, jnp.float32) + bias.astype(jnp.float32)[None, :]
    for offset in range(taps):
        lag = taps - 1 - offset
        source = document_of(positions - lag, doc_lengths)
        same = (source == doc_ids).astype(jnp.float32)
        total = (
            total
            + weight[offset].astype(jnp.float32)[None, :]
            * joined[offset : offset + length]
            * same[:, None]
        )
    return jax.nn.silu(total).astype(jnp.bfloat16)


def span_step(state, pieces, rates):
    signal, bmat, cmat, steps, doc_ids, doc_prev = pieces
    signal = signal.astype(jnp.float32)
    bmat = bmat.astype(jnp.float32)
    cmat = cmat.astype(jnp.float32)
    climb = jnp.cumsum(steps * rates[:, None], axis=1)
    extent = doc_ids.shape[0]
    order = jnp.arange(extent, dtype=jnp.int32)
    inside = (doc_ids[:, None] == doc_ids[None, :]) & (order[:, None] >= order[None, :])
    gap = climb[:, :, None] - climb[:, None, :]
    decay = jnp.where(inside[None], jnp.exp(-jnp.where(inside[None], gap, 0.0)), 0.0)
    scores = jnp.dot(cmat, bmat.T, precision=HIGH)
    weights = decay * scores[None] * steps[:, None, :]
    output = jnp.einsum("hts,shp->thp", weights, signal, precision=HIGH)
    carried = (doc_ids == doc_prev).astype(jnp.float32)
    entry = jnp.exp(-climb) * carried[None, :]
    output = output + jnp.einsum("tn,hpn->thp", cmat, state, precision=HIGH) * entry.T[:, :, None]
    last = doc_ids[extent - 1]
    tail = (
        jnp.exp(climb - climb[:, extent - 1 :])
        * (doc_ids == last).astype(jnp.float32)[None, :]
        * steps
    )
    kept = jnp.exp(-climb[:, extent - 1]) * (last == doc_prev).astype(jnp.float32)
    fresh = jnp.einsum("hs,shp,sn->hpn", tail, signal, bmat, precision=HIGH)
    return (kept[:, None, None] * state + fresh, output)


def chain_combine(earlier, later):
    return (earlier[0] * later[0], later[0][:, None, None] * earlier[1] + later[1])


def softmax_combine(first_part, second_part):
    peak = jnp.maximum(first_part[0], second_part[0])
    total = first_part[1] * jnp.exp(first_part[0] - peak) + second_part[1] * jnp.exp(
        second_part[0] - peak
    )
    return (peak, total, first_part[2] + second_part[2])


def local(
    residual,
    x_in,
    bc_in,
    z_in,
    dt_raw,
    dt_bias,
    decay_rate,
    d_skip,
    conv_x_weight,
    conv_x_bias,
    conv_bc_weight,
    conv_bc_bias,
    norm_gain,
    out_weight,
    final_gain,
    lm_weight,
    targets,
    doc_lengths,
):
    length = x_in.shape[0]
    inner_here = x_in.shape[1]
    heads_here = dt_raw.shape[0]
    seq_rank = lax.axis_index("seq")
    head_rank = lax.axis_index("head")
    offset_here = seq_rank * length
    positions = offset_here + jnp.arange(length, dtype=jnp.int32)
    doc_ids = document_of(positions, doc_lengths)
    margin = KERNEL - 1
    x_rim, bc_rim = shifted((x_in[length - margin :], bc_in[length - margin :]), "seq", 1)
    signal = causal_conv(x_in, x_rim, conv_x_weight, conv_x_bias, positions, doc_ids, doc_lengths)
    keys_queries = causal_conv(
        bc_in, bc_rim, conv_bc_weight, conv_bc_bias, positions, doc_ids, doc_lengths
    )
    steps = jax.nn.softplus(dt_raw + dt_bias[:, None])
    blocks = length // SPAN
    block_starts = offset_here + jnp.arange(blocks, dtype=jnp.int32) * SPAN
    pieces = (
        signal.reshape(blocks, SPAN, heads_here, HEAD_SIZE),
        keys_queries[:, :STATE].reshape(blocks, SPAN, STATE),
        keys_queries[:, STATE:].reshape(blocks, SPAN, STATE),
        steps.reshape(heads_here, blocks, SPAN).transpose(1, 0, 2),
        doc_ids.reshape(blocks, SPAN),
        document_of(block_starts - 1, doc_lengths),
    )

    def advance(state, piece):
        return span_step(state, piece, decay_rate)

    local_end, outputs = lax.scan(
        advance, jnp.zeros((heads_here, HEAD_SIZE, STATE), jnp.float32), pieces
    )
    outputs = outputs.reshape(length, heads_here, HEAD_SIZE)
    before = document_of(jnp.reshape(offset_here - 1, (1,)), doc_lengths)[0]
    carried = (doc_ids == before).astype(jnp.float32)
    climb = jnp.cumsum(steps * decay_rate[:, None], axis=1)
    through = jnp.exp(-climb[:, length - 1]) * carried[length - 1]
    identity = (jnp.ones_like(through), jnp.zeros_like(local_end))
    incoming = entering((through, local_end), "seq", chain_combine, identity)[1]
    entry = jnp.exp(-climb) * carried[None, :]
    cmat = keys_queries[:, STATE:].astype(jnp.float32)
    outputs = (
        outputs + jnp.einsum("tn,hpn->thp", cmat, incoming, precision=HIGH) * entry.T[:, :, None]
    )
    mixed = outputs + d_skip[None, :, None] * signal.reshape(length, heads_here, HEAD_SIZE).astype(
        jnp.float32
    )
    gated = mixed.reshape(length, inner_here) * jax.nn.silu(z_in.astype(jnp.float32))
    square_sum = lax.psum(jnp.sum(gated * gated, axis=1), "head")
    scale = lax.rsqrt(square_sum / INNER + EPSILON)
    normed = (gated * scale[:, None] * norm_gain.astype(jnp.float32)[None, :]).astype(jnp.bfloat16)
    partial_value = jnp.dot(normed, out_weight, preferred_element_type=jnp.float32)
    share = residual.shape[1]
    projected = sent_and_summed(partial_value, "head", 1)
    block_out = (residual.astype(jnp.float32) + projected).astype(jnp.bfloat16)
    widened = block_out.astype(jnp.float32)
    square_total = lax.psum(jnp.sum(widened * widened, axis=1), "head")
    gain_part = lax.dynamic_slice_in_dim(final_gain, head_rank * share, share, 0)
    final_scale = lax.rsqrt(square_total / D + EPSILON)
    hidden_part = (widened * final_scale[:, None] * gain_part.astype(jnp.float32)[None, :]).astype(
        jnp.bfloat16
    )
    hidden = gather_directly(hidden_part, "head", 1)
    vocab_here = lm_weight.shape[1]
    logits = jnp.dot(
        hidden,
        lax.all_gather(lm_weight, "seq", axis=0, tiled=True),
        preferred_element_type=jnp.float32,
    )
    peak = jnp.max(logits, axis=1)
    total = jnp.sum(jnp.exp(logits - peak[:, None]), axis=1)
    local_target = targets - head_rank * vocab_here
    column = jnp.arange(vocab_here, dtype=jnp.int32)
    picked = jnp.sum(jnp.where(column[None, :] == local_target[:, None], logits, 0.0), axis=1)
    peak_all, total_all, picked_all = joined_2((peak, total, picked), "head", softmax_combine)
    losses = peak_all + jnp.log(total_all) - picked_all
    member = (
        doc_ids[:, None] == jnp.arange(doc_lengths.shape[0], dtype=jnp.int32)[None, :]
    ).astype(jnp.float32)
    sums = over_copies(jnp.dot(losses, member, precision=HIGH), "seq")
    return (block_out, sums / doc_lengths.astype(jnp.float32))


def solution(mesh):
    in_specs = (
        P(("groups", "seq"), "head"),
        P(("groups", "seq"), "head"),
        P(("groups", "seq"), None),
        P(("groups", "seq"), "head"),
        P("head", ("groups", "seq")),
        P("head"),
        P("head"),
        P("head"),
        P(None, "head"),
        P("head"),
        P(),
        P(),
        P("head"),
        P("head", None),
        P(),
        P("seq", "head"),
        P(("groups", "seq")),
        P("groups"),
    )
    out_specs = (P(("groups", "seq"), "head"), P("groups"))
    return jax.shard_map(local, mesh=mesh, in_specs=in_specs, out_specs=out_specs, check_vma=False)
```

profile of v0, /device:TPU:40, one launch (start us, length us, event | category | flops | bytes accessed | tf_op | source)
XLA Modules:
  0.0 453.5 jit_solution(4214907796771070101)
XLA Ops:
  7.3 1.5 slice.103
  8.7 5.3 %collective-permute-start = (bf16[3,640]{1,0:T(4,128)(2,1)}, bf16[3,640]{1,0:T(4,128)(2,1)}, u32[]{:S(2)}, u32[]{:S(2)}) collective-permute-start(bf16[3,640]{1,0:T(4,128)(2,1)} %slice.103), channel_id=1, source_target_pairs={{0,8},{8,16},{16,24},{24,32},{32,40},{40,48},{48,56},{56,64},{64,7... | collective-permute-start | bytes 11528 | tf_op jit(solution)/shard_map/ppermute | solution.py:21
  14.7 4.1 collective-permute-start.1
  19.8 1.3 fusion.83
  21.7 0.8 slice_convert_fusion.3
  23.4 1.5 broadcast_multiply_fusion.1
  25.4 1.5 convert_reduce_fusion.7
  29.4 1.0 maximum_convert_fusion.1
  31.5 0.8 maximum_convert_fusion
  32.4 1.9 multiply_convert_fusion.1
  34.3 2.2 copy.83
  36.5 2.7 reshape.293
  39.1 2.1 copy.85
  41.2 80.0 %while.46 = (s32[]{:T(128)}, f32[10,64,128]{2,1,0:T(8,128)}, f32[2,256,10,64]{1,0,3,2:T(2,128)}, f32[2,10,256]{2,0,1:T(2,128)}, f32[10]{0:T(128)}, /*index=5*/s3...) while((s32[]{:T(128)}, f32[10,64,128]{2,1,0:T(8,128)}, ...), condition=%wide.region_9.10_spmd.clone, body=%wide.region_6.9_spmd.clone.sunk | while | flops 1028866112 | bytes 7581990 | solution.py:210
  43.3 1.9 reduce-window.36
  45.1 1.4 slice_reduce_fusion.5
  48.0 1.3 dynamic_slice.148
  49.3 1.8 compare_convert_fusion.7
  51.4 4.0 fusion.117
  55.4 1.3 dynamic-slice.6
  57.4 0.9 slice_reduce_fusion.6
  58.3 1.4 multiply_bitcast_fusion.4
  59.7 1.5 fusion.118
  61.3 1.5 copy.129
  62.8 14.2 %dynamic_update_slice.6 = f32[2,256,10,64]{1,0,3,2:T(2,128)} dynamic-update-slice(f32[2,256,10,64]{1,0,3,2:T(2,128)} %get-tuple-element.624, f32[1,256,10,64]{1,0,3,2:T(1,128)} %copy.129, s32[]{:T(128)} %get-tuple-element.622, s32[]{:T(128)} %constant.152.clone.1..sunk.2, s32[]{:T(128)} %constant.152.clone.1..sunk.2, s32[]{:T(128)} %constant.152.clone.1..sunk.2) | dynamic-update-slice | bytes 1310724 | tf_op jit(solution)/shard_map/while/body/jit(dynamic_update_index_in_dim)/dynamic_update_slice | solution.py:210
  78.9 2.2 convolution_add_fusion.2
  83.2 1.9 reduce-window.36
  85.0 1.4 slice_reduce_fusion.5
  87.1 0.8 broadcast_add_fusion.5
  87.9 1.3 dynamic_slice.148
  89.2 1.8 compare_convert_fusion.7
  91.3 4.0 fusion.117
  95.3 1.3 dynamic-slice.6
  97.3 0.9 slice_reduce_fusion.6
  98.2 1.4 multiply_bitcast_fusion.4
  99.6 1.6 fusion.118
  101.2 1.5 copy.129
  102.8 14.2 %dynamic_update_slice.6 = f32[2,256,10,64]{1,0,3,2:T(2,128)} dynamic-update-slice(f32[2,256,10,64]{1,0,3,2:T(2,128)} %get-tuple-element.624, f32[1,256,10,64]{1,0,3,2:T(1,128)} %copy.129, s32[]{:T(128)} %get-tuple-element.622, s32[]{:T(128)} %constant.152.clone.1..sunk.2, s32[]{:T(128)} %constant.152.clone.1..sunk.2, s32[]{:T(128)} %constant.152.clone.1..sunk.2) | dynamic-update-slice | bytes 1310724 | tf_op jit(solution)/shard_map/while/body/jit(dynamic_update_index_in_dim)/dynamic_update_slice | solution.py:210
  118.9 2.3 convolution_add_fusion.2
  122.7 1.2 reduce-window.30
  126.5 44.9 %all-reduce = f32[160]{0:T(256)S(1)} all-reduce(f32[160]{0:T(256)S(1)} %dynamic-update-slice), channel_id=2, replica_groups=mesh['groups'=2,'seq'=16,'head'=8] {'seq'}, use_global_device_ids=true, to_apply=%add | all-reduce | flops 160 | bytes 1280
  172.1 2.4 copy.89
  174.5 3.2 reshape.296
  177.7 34.0 %all-gather.9.cloned.1.call-done = f32[160,64,128]{2,1,0:T(8,128)} async-done(((f32[10,64,128]{2,1,0:T(8,128)}), f32[160,64,128]{2,1,0:T(8,128)}) %all-gather.9.cloned.1.call-update) | async-done | bytes 5242896 | tf_op jit(solution)/shard_map/all_gather | solution.py:26
  212.5 0.9 copy-done.4
  213.5 3.7 fusion.46
  217.2 2.8 copy.90
  220.0 2.0 multiply_reduce_fusion
  222.0 12.9 %psum.14 = f32[512]{0:T(512)S(1)} all-reduce(f32[512]{0:T(512)S(1)} %multiply_reduce_fusion), channel_id=1, replica_groups=mesh['groups'=2,'seq'=16,'head'=8] {'head'}, use_global_device_ids=true, to_apply=%region_16.17 | all-reduce | flops 512 | bytes 4096 | tf_op jit(solution)/shard_map/psum | solution.py:229
  234.9 6.4 %fusion.61 = f32[512,2560]{0,1:T(8,128)} fusion(bf16[640,2560]{1,0:T(8,128)(2,1)S(1)} %copy-done, f32[640]{0:T(1024)S(1)} %convert_element_type.158, f32[512]{0:T(512)S(1)} %add_rsqrt_fusion.1, f32[512,640]{1,0:T(8,128)} %copy.90, bf16[512,640]{1,0:T(8,128)(2,1)} %param.27), kind=kOutput, calls=%fused_computation.97 | convolution fusion | flops 1680670720 | bytes 10490368 | tf_op jit(solution)/shard_map/dot_general | solution.py:232
  241.3 4.9 %all-to-all-start = ((f32[8,512,320]{1,2,0:T(8,128)}), f32[8,512,320]{1,2,0:T(8,128)}, u32[]{:S(2)}, u32[]{:S(2)}) async-start(f32[8,512,320]{1,2,0:T(8,128)} %bitcast.151), calls=%async_computation | async-start | bytes 10485760 | tf_op jit(solution)/shard_map/all_to_all | solution.py:45
  246.9 60.0 %all-to-all-done = f32[8,512,320]{1,2,0:T(8,128)} async-done(((f32[8,512,320]{1,2,0:T(8,128)}), f32[8,512,320]{1,2,0:T(8,128)}, u32[]{:S(2)}, u32[]{:S(2)}) %all-to-all-start) | async-done | bytes 5242912 | tf_op jit(solution)/shard_map/all_to_all | solution.py:45
  306.9 4.1 reduce_sum.118
  310.9 2.0 fusion.58
  312.9 13.5 %psum.15 = f32[512]{0:T(512)S(1)} all-reduce(f32[512]{0:T(512)S(1)} %get-tuple-element.424), channel_id=1, replica_groups=mesh['groups'=2,'seq'=16,'head'=8] {'head'}, use_global_device_ids=true, to_apply=%region_19.20 | all-reduce | flops 512 | bytes 4096 | tf_op jit(solution)/shard_map/psum | solution.py:237
  326.5 1.1 fusion.60
  327.6 1.7 broadcast_in_dim.26
  329.3 4.7 %all-to-all-start.1 = ((bf16[8,512,320]{1,2,0:T(8,128)(2,1)}), bf16[8,512,320]{1,2,0:T(8,128)(2,1)}, u32[]{:S(2)}, u32[]{:S(2)}) async-start(bf16[8,512,320]{1,2,0:T(8,128)(2,1)} %broadcast_in_dim.26), calls=%async_computation.1 | async-start | bytes 5242880 | tf_op jit(solution)/shard_map/all_to_all | solution.py:57
  334.0 32.6 %all-to-all-done.1 = bf16[8,512,320]{1,2,0:T(8,128)(2,1)} async-done(((bf16[8,512,320]{1,2,0:T(8,128)(2,1)}), bf16[8,512,320]{1,2,0:T(8,128)(2,1)}, u32[]{:S(2)}, u32[]{:S(2)}) %all-to-all-start.1) | async-done | bytes 2621472 | tf_op jit(solution)/shard_map/all_to_all | solution.py:57
  366.7 27.4 %all-gather.7.cloned.1.call-done = bf16[2560,3200]{1,0:T(8,128)(2,1)} async-done(((bf16[160,3200]{1,0:T(8,128)(2,1)}), bf16[2560,3200]{1,0:T(8,128)(2,1)}) %all-gather.7.cloned.1.call-update) | async-done | bytes 16384016 | tf_op jit(solution)/shard_map/all_gather | solution.py:247
  394.1 14.5 %fusion.89 = (f32[512]{0:T(512)S(1)}, f32[512,3200]{1,0:T(8,128)S(1)}) fusion(bf16[512,2560]{0,1:T(8,128)(2,1)} %bitcast.23, bf16[2560,3200]{1,0:T(8,128)(2,1)} %all-gather.7.cloned.1.call-done), kind=kOutput, calls=%fused_computation.170 | convolution fusion | flops 8390245888 | bytes 25561088 | tf_op jit(solution)/shard_map/dot_general | solution.py:245
  408.6 2.0 exponential_reduce_fusion
  410.6 13.2 %all-gather.3 = f32[8,3,512]{2,1,0:T(4,128)S(1)} all-gather(f32[1,3,512]{2,1,0:T(4,128)S(1)} %maximum_bitcast_fusion), channel_id=4, replica_groups=mesh['groups'=2,'seq'=16,'head'=8] {'head'}, dimensions={0}, use_global_device_ids=true | all-gather | bytes 55296 | tf_op jit(solution)/shard_map/all_gather | solution.py:74
  424.9 21.2 %all_to_all.16 = f32[16,1,16]{2,1,0:T(1,128)S(1)} all-to-all(f32[16,1,16]{2,1,0:T(1,128)S(1)} %broadcast_in_dim.28), channel_id=1, replica_groups=mesh['groups'=2,'seq'=16,'head'=8] {'seq'}, dimensions={0} | all-to-all | bytes 2048 | tf_op jit(solution)/shard_map/all_to_all | solution.py:57
  (161 shorter events, 23.6 us)
Async XLA Ops:
  7.2 227.7 %copy-start = (bf16[640,2560]{1,0:T(8,128)(2,1)S(1)}, bf16[640,2560]{1,0:T(8,128)(2,1)}, u32[]{:S(2)}) copy-start(bf16[640,2560]{1,0:T(8,128)(2,1)} %param.37) | copy-start | bytes 9830404
  7.2 204.6 %all-gather.9.cloned.1.call-start = ((), (), s32[]{:S(2)}) async-start(), calls=%async_computation.4 | async-start | bytes 5570560 | tf_op jit(solution)/shard_map/all_gather | solution.py:26
  8.7 22.8 %collective-permute-start = (bf16[3,640]{1,0:T(4,128)(2,1)}, bf16[3,640]{1,0:T(4,128)(2,1)}, u32[]{:S(2)}, u32[]{:S(2)}) collective-permute-start(bf16[3,640]{1,0:T(4,128)(2,1)} %slice.103), channel_id=1, source_target_pairs={{0,8},{8,16},{16,24},{24,32},{32,40},{40,48},{48,56},{56,64},{64,7... | collective-permute-start | bytes 11528 | tf_op jit(solution)/shard_map/ppermute | solution.py:21
  14.7 14.7 %collective-permute-start.1 = (bf16[3,256]{1,0:T(4,128)(2,1)S(1)}, bf16[3,256]{1,0:T(4,128)(2,1)S(1)}, u32[]{:S(2)}, u32[]{:S(2)}) collective-permute-start(bf16[3,256]{1,0:T(4,128)(2,1)S(1)} %slice.112), channel_id=1, source_target_pairs={{0,8},{8,16},{16,24},{24,32},{32,40},{40,48},{48,56},{56,64},{64,7... | collective-permute-start | bytes 4616 | tf_op jit(solution)/shard_map/ppermute | solution.py:21
  22.7 7.7 %copy-start.13 = (s32[512]{0:T(512)}, s32[512]{0:T(512)S(1)}, u32[]{:S(2)}) copy-start(s32[512]{0:T(512)S(1)} %broadcast_add_fusion.2) | copy-start | bytes 6148
  30.4 1.1 copy-start.5
  30.8 0.7 copy-start.3
  30.8 1.5 copy-start.8
  30.8 1.5 copy-start.9
  30.9 1.5 copy-start.10
  30.9 1.5 copy-start.11
  48.0 3.4 copy-start.1
  58.3 1.4 copy-start.7
  61.2 17.7 %copy-start.2 = (f32[256,10]{0,1:T(8,128)S(1)}, f32[256,10]{0,1:T(8,128)}, u32[]{:S(2)}) copy-start(f32[256,10]{0,1:T(8,128)} %get-tuple-element.606) | copy-start | bytes 30724 | tf_op jit(solution)/shard_map/while
  87.9 3.4 copy-start.1
  98.2 1.4 copy-start.7
  101.2 17.7 %copy-start.2 = (f32[256,10]{0,1:T(8,128)S(1)}, f32[256,10]{0,1:T(8,128)}, u32[]{:S(2)}) copy-start(f32[256,10]{0,1:T(8,128)} %get-tuple-element.606) | copy-start | bytes 30724 | tf_op jit(solution)/shard_map/while
  121.2 0.9 copy-start.12
  121.2 1.5 copy-start.6
  121.2 3.0 copy-start.19
  121.2 50.3 %copy-start.15 = (bf16[640]{0:T(1024)(128)(2,1)S(1)}, bf16[640]{0:T(1024)(128)(2,1)}, u32[]{:S(2)}) copy-start(bf16[640]{0:T(1024)(128)(2,1)} %param.36) | copy-start | bytes 3844
  121.2 272.9 %all-gather.7.cloned.1.call-start = ((), (), s32[]{:S(2)}) async-start(), calls=%async_computation.3 | async-start | bytes 17408000 | tf_op jit(solution)/shard_map/all_gather | solution.py:247
  212.5 0.9 copy-start.4
  212.5 1.0 copy-start.18
  241.3 65.6 %all-to-all-start = ((f32[8,512,320]{1,2,0:T(8,128)}), f32[8,512,320]{1,2,0:T(8,128)}, u32[]{:S(2)}, u32[]{:S(2)}) async-start(f32[8,512,320]{1,2,0:T(8,128)} %bitcast.151), calls=%async_computation | async-start | bytes 10485760 | tf_op jit(solution)/shard_map/all_to_all | solution.py:45
  329.3 4.7 %copy-start.17 = (s32[512]{0:T(512)S(1)}, s32[512]{0:T(512)}, u32[]{:S(2)}) copy-start(s32[512]{0:T(512)} %param.40) | copy-start | bytes 6148
  329.3 37.4 %all-to-all-start.1 = ((bf16[8,512,320]{1,2,0:T(8,128)(2,1)}), bf16[8,512,320]{1,2,0:T(8,128)(2,1)}, u32[]{:S(2)}, u32[]{:S(2)}) async-start(bf16[8,512,320]{1,2,0:T(8,128)(2,1)} %broadcast_in_dim.26), calls=%async_computation.1 | async-start | bytes 5242880 | tf_op jit(solution)/shard_map/all_to_all | solution.py:57
  408.6 16.0 %copy-start.14 = (s32[512]{0:T(512)S(1)}, s32[512]{0:T(512)}, u32[]{:S(2)}) copy-start(s32[512]{0:T(512)} %copy-done.13) | copy-start | bytes 6148
  408.6 37.5 %copy-start.16 = (s32[16]{0:T(128)S(1)}, s32[16]{0:T(128)}, u32[]{:S(2)}) copy-start(s32[16]{0:T(128)} %param.41) | copy-start | bytes 196
Sparse Core Ops, SparseCore 0:
  121.4 90.3 all-gather.8
  213.6 180.4 all-gather.6
where the time goes:
time: 458 us; the launch traced here: 454 us
  waiting for transfers between devices  155 us (34%)
  blocking collectives  106 us (23%)
  local copies, waits for them, and re-layouts  69.2 us (15%)
  other arithmetic  44.6 us (10%)
  matrix products  40.9 us (9%)
  starting transfers between devices  19.1 us (4%)
  between operations  15.8 us (3%)
    all_to_all x1, waiting for transfers between devices, sent_and_summed(): lax.all_to_all(blocks, axis, split_axis=0, concat_axis=0, tiled=True)  60 us
    unnamed x1, blocking collectives  44.9 us
    all_gather x1, waiting for transfers between devices, entering(): gathered = jax.tree.map(lambda a: lax.all_gather(a, axis), part)  34 us
    all_to_all x1, waiting for transfers between devices, from_everyone(): lax.all_to_all(jnp.broadcast_to(array[None], (length, *array.shape)), axi...  32.6 us
    dynamic_update_slice x4, local copies, waits for them, and re-layouts, local(): lax.scan(advance, jnp.zeros((heads_here, HEAD_SIZE, STATE), jnp.float32),...  31.3 us
    all_gather x1, waiting for transfers between devices, local(): lax.all_gather(lm_weight, 'seq', axis=0, tiled=True)  27.4 us
    all_to_all x1, blocking collectives, from_everyone(): lax.all_to_all(jnp.broadcast_to(array[None], (length, *array.shape)), axi...  21.2 us
    dot_general x1, matrix products, local(): jnp.dot(hidden, lax.all_gather(lm_weight, 'seq', axis=0, tiled=True), pre...  14.5 us
  transfers between devices with their start and end apart: 6, of which 4 were waited for; matrix products, arithmetic and copies ran while one was open for 10% of the time, Pallas kernels for 0%

commit v1 on v0

v1 whole, which is shorter than its diff:
```python
import functools

import jax
import jax.numpy as jnp
from jax import lax
from jax.experimental import pallas as pl
from jax.experimental.pallas import tpu as pltpu
from jax.sharding import Mesh
from jax.sharding import PartitionSpec as P

STATE = 128
HEAD_SIZE = 64
KERNEL = 4
LONGEST = 1536
EPSILON = 1e-05
LANES = 128
RIM = 8
NEG = -1e30
F32 = jnp.float32
BF16 = jnp.bfloat16

SMEM = pl.BlockSpec(memory_space=pltpu.SMEM)
HEADS_AXES = ("x", "core")


def dot(a, b, ca=1, cb=0):
    return lax.dot_general(a, b, (((ca,), (cb,)), ((), ())), preferred_element_type=F32)


def in_two(value):
    high = value.astype(BF16)
    return high, (value - high.astype(F32)).astype(BF16)


def in_three(value):
    high = value.astype(BF16)
    rest = value - high.astype(F32)
    middle = rest.astype(BF16)
    return high, middle, (rest - middle.astype(F32)).astype(BF16)


def silu(value):
    return value * jax.nn.sigmoid(value)


def starts_of(lens):
    start = jnp.int32(0)
    for d in range(lens.shape[0]):
        yield start
        start = start + lens[d]


def own_starts(lens, offset, length):
    pos = offset + lax.broadcasted_iota(jnp.int32, (length, LANES), 0)
    found = jnp.zeros((length, LANES), jnp.int32)
    for start in starts_of(lens):
        found = jnp.where(pos >= start, start, found)
    return pos, found


def pair_of(cols, at):
    lane = lax.broadcasted_iota(jnp.int32, (cols.shape[0], LANES), 1)
    return jnp.where(lane < HEAD_SIZE, cols[:, at : at + 1], cols[:, at + 1 : at + 2])


def front_kernel(
    lens, offset_ref, x_ref, xr_ref, bc_ref, bcr_ref, dt_ref, hp_ref, cw_ref, cb_ref, bw_ref, bb_ref,
    val_ref, kq_ref, cols_ref, rows_ref, e_ref, d_ref, xs, bs, rs,
):
    length, width = x_ref.shape
    heads = dt_ref.shape[0]
    offset = offset_ref[0]
    pos, found = own_starts(lens, offset, length)
    depth = pos - found
    last_start = jnp.int32(0)
    first_here = jnp.int32(2**30)
    for start in starts_of(lens):
        last_start = jnp.where(start <= offset + length - 1, start, last_start)
        first_here = jnp.where(start >= offset, jnp.minimum(first_here, start), first_here)

    bs[:RIM] = bcr_ref[...].astype(F32)
    bs[RIM:] = bc_ref[...].astype(F32)
    xs[:RIM] = xr_ref[...].astype(F32)
    xs[RIM:] = x_ref[...].astype(F32)

    def conv(buf, w_ref, b_ref, at):
        sl = slice(at, at + LANES)
        total = jnp.zeros((length, LANES), F32) + b_ref[:, sl].astype(F32)
        for k in range(KERNEL):
            lag = KERNEL - 1 - k
            tap = w_ref[k : k + 1, sl].astype(F32) * buf[RIM - lag : RIM - lag + length, sl]
            total = total + (jnp.where(depth >= lag, tap, 0.0) if lag else tap)
        return silu(total).astype(BF16)

    for at in range(0, 2 * STATE, LANES):
        kq_ref[:, at : at + LANES] = conv(bs, bw_ref, bb_ref, at)

    hp = hp_ref[...]
    raw = dt_ref[...] + hp[:, 0:1]
    steps = jnp.maximum(raw, 0.0) + jnp.log1p(jnp.exp(-jnp.abs(raw)))
    rates = steps * hp[:, 1:2]
    upper = (
        lax.broadcasted_iota(jnp.int32, (length, length), 0)
        <= lax.broadcasted_iota(jnp.int32, (length, length), 1)
    ).astype(F32).astype(BF16)
    high, middle, low = in_three(rates)
    climb = dot(low, upper) + dot(middle, upper) + dot(high, upper)
    end = climb[:, length - 1 :]
    spot = lax.broadcasted_iota(jnp.int32, (heads, length), 1)
    tail = jnp.where(spot >= last_start - offset, jnp.exp(climb - end) * steps, 0.0)
    entry = jnp.where(spot < first_here - offset, jnp.exp(-climb), 0.0)
    rs[...] = jnp.zeros(rs.shape, F32)
    rs[0:heads] = climb
    rs[16 : 16 + heads] = tail
    rs[32 : 32 + heads] = entry
    cols = rs[...].T
    cols_ref[...] = cols
    rows_ref[...] = jnp.zeros(rows_ref.shape, F32)
    rows_ref[0:heads] = climb
    rows_ref[16 : 16 + heads] = steps
    keys = kq_ref[:, :STATE].astype(F32).T.astype(BF16)
    for j in range(width // LANES):
        sl = slice(j * LANES, (j + 1) * LANES)
        value = conv(xs, cw_ref, cb_ref, j * LANES)
        val_ref[:, sl] = value
        high, low = in_two(value.astype(F32) * pair_of(cols, 16 + 2 * j))
        e_ref[:, sl] = dot(keys, high) + dot(keys, low)
        d_ref[:, sl] = pair_of(cols[length - 8 :], 32 + 2 * j)


def intra_kernel(lens, offset_ref, kq_ref, val_ref, cols_ref, rows_ref, y_ref):
    length, width = val_ref.shape
    offset = offset_ref[0]
    _, found = own_starts(lens, offset, length)
    found = found - offset
    lane = lax.broadcasted_iota(jnp.int32, (LANES, LANES), 1)
    for i in range(length // LANES):
        rows = slice(i * LANES, (i + 1) * LANES)
        upto = (i + 1) * LANES
        scores = dot(kq_ref[rows, STATE:], kq_ref[:upto, :STATE], 1, 1)
        t = i * LANES + lax.broadcasted_iota(jnp.int32, (LANES, upto), 0)
        s = lax.broadcasted_iota(jnp.int32, (LANES, upto), 1)
        scores = jnp.where((s <= t) & (s >= found[rows, 0:1]), scores, 0.0)
        for j in range(width // LANES):
            sl = slice(j * LANES, (j + 1) * LANES)
            both = []
            for h in (2 * j, 2 * j + 1):
                gap = rows_ref[h : h + 1, :upto] - cols_ref[rows, h : h + 1]
                weight = jnp.exp(jnp.minimum(gap, 0.0)) * scores * rows_ref[16 + h : 17 + h, :upto]
                high, low = in_two(weight)
                both.append(dot(high, val_ref[:upto, sl]) + dot(low, val_ref[:upto, sl]))
            y_ref[rows, sl] = jnp.where(lane < HEAD_SIZE, both[0], both[1])


def gate_kernel(kq_ref, s_ref, cols_ref, y_ref, val_ref, z_ref, skip_ref, g_ref, ss_ref):
    length, width = val_ref.shape
    cols = cols_ref[...]
    total = jnp.zeros((length, LANES), F32)
    for j in range(width // LANES):
        sl = slice(j * LANES, (j + 1) * LANES)
        high, low = in_two(s_ref[:, sl])
        far = dot(kq_ref[:, STATE:], high) + dot(kq_ref[:, STATE:], low)
        out = y_ref[:, sl] + far * pair_of(cols, 32 + 2 * j)
        mixed = out + skip_ref[:, sl] * val_ref[:, sl].astype(F32)
        gated = mixed * silu(z_ref[:, sl].astype(F32))
        g_ref[:, sl] = gated
        total = total + gated * gated
    ss_ref[...] = jnp.sum(total.T, axis=0, keepdims=True)


def project_first_kernel(order, w_ref, p0, p1, p2, p3, p4, p5, acc_ref):
    total = jnp.zeros(acc_ref.shape, F32)
    for k, piece in enumerate((p0, p1, p2, p3, p4, p5)):
        total = total + dot(w_ref[order[k]], piece[...], 1, 1)
    acc_ref[...] = total


def project_last_kernel(order, w_ref, acc_ref, res_ref, a0, b0, a1, b1, out_ref):
    half = a0.shape[0]
    for at, pieces in ((0, (a0, a1)), (half, (b0, b1))):
        sl = slice(at, at + half)
        total = acc_ref[:, sl]
        for k, piece in enumerate(pieces):
            total = total + dot(w_ref[order[6 + k]], piece[...], 1, 1)
        out_ref[:, sl] = (res_ref[:, sl].astype(F32) + total).astype(BF16)


def logits_kernel(order, meta, *refs, members, overlap):
    per = 10
    pieces = [refs[m * per : (m + 1) * per] for m in range(members)]
    gain_ref, target_ref, w_ref, out_ref, wide, hid, peak, total, pick, want = refs[members * per :]
    step = pl.program_id(0)
    block = w_ref.shape[1]
    depth = wide.shape[0]
    length = wide.shape[1]
    rows = members * length

    @pl.when(step == 0)
    def _():
        for m in range(members):
            part = pieces[m][0].shape[0]
            squares = jnp.zeros((1, length), F32)
            for k in range(6):
                piece = pieces[m][k][...]
                at = pl.multiple_of(order[k] * part, 64)
                wide[pl.ds(at, part), :] = piece
                big = piece.astype(F32)
                squares = squares + jnp.sum(big * big, axis=0, keepdims=True)
            for k in range(2):
                at = pl.multiple_of(order[6 + k] * part, 64)
                piece = jnp.concatenate([pieces[m][6 + 2 * k][...], pieces[m][7 + 2 * k][...]], axis=1)
                wide[pl.ds(at, part), :] = piece
                big = piece.astype(F32)
                squares = squares + jnp.sum(big * big, axis=0, keepdims=True)
            scale = lax.rsqrt(squares / depth + EPSILON)
            for at in range(0, depth, LANES):
                sl = slice(at, at + LANES)
                value = wide[sl, :].astype(F32) * scale * gain_ref[sl, :]
                hid[m * length : (m + 1) * length, sl] = value.T.astype(BF16)
        want[...] = jnp.zeros((rows, LANES), jnp.int32) + target_ref[...]
        peak[...] = jnp.full((rows, LANES), NEG, F32)
        total[...] = jnp.zeros((rows, LANES), F32)
        pick[...] = jnp.zeros((rows, LANES), F32)

    chunk = 256
    for r in range(0, rows, chunk):
        rw = slice(r, r + chunk)
        logits = dot(hid[rw, :], w_ref[...])
        lane = lax.broadcasted_iota(jnp.int32, (chunk, LANES), 1)
        groups = []
        found = pick[rw, :]
        old = peak[rw, :]
        top = old
        for g in range(block // LANES):
            at = step * block + g * LANES
            part = logits[:, g * LANES : (g + 1) * LANES]
            good = (meta[0] == 0) | (at >= overlap)
            part = jnp.where(good, part, NEG)
            groups.append(part)
            found = found + jnp.where((lane + (at + meta[1]) == want[rw, :]) & good, part, 0.0)
            top = jnp.maximum(top, part)
        add = total[rw, :] * jnp.exp(old - top)
        for part in groups:
            add = add + jnp.exp(part - top)
        pick[rw, :] = found
        peak[rw, :] = top
        total[rw, :] = add

    @pl.when(step == pl.num_programs(0) - 1)
    def _():
        tops = peak[...].T
        top = jnp.max(tops, axis=0, keepdims=True)
        out_ref[0:1, :] = top + jnp.log(jnp.sum(total[...].T * jnp.exp(tops - top), axis=0, keepdims=True))
        out_ref[1:2, :] = jnp.sum(pick[...].T, axis=0, keepdims=True)


def shape(dims, dtype):
    return jax.ShapeDtypeStruct(dims, dtype)


def cost(flops, nbytes):
    return pl.CostEstimate(flops=int(flops), bytes_accessed=int(nbytes), transcendentals=0)


def ring(length, by):
    return [(i, (i + by) % length) for i in range(length)]


def swapped(length, bit):
    return [(i, i ^ bit) for i in range(length)]


def around_x(piece, dim):
    size = lax.axis_size("x")
    half = piece.shape[dim] // 2
    left = lax.ppermute(piece, "x", ring(size, 1))
    right = lax.ppermute(piece, "x", ring(size, -1))
    own_other = lax.ppermute(piece, "core", swapped(2, 1))
    far_a = lax.ppermute(lax.slice_in_dim(left, 0, half, axis=dim), "x", ring(size, 1))
    far_b = lax.ppermute(lax.slice_in_dim(right, half, 2 * half, axis=dim), "x", ring(size, -1))
    left_other = lax.ppermute(left, "core", swapped(2, 1))
    right_other = lax.ppermute(right, "core", swapped(2, 1))
    far_a_other = lax.ppermute(far_a, "core", swapped(2, 1))
    far_b_other = lax.ppermute(far_b, "core", swapped(2, 1))
    near = (piece, own_other, left, left_other, right, right_other)
    return near, (far_a, far_b, far_a_other, far_b_other)


def order_here():
    size = lax.axis_size("x")
    x, core = lax.axis_index("x"), lax.axis_index("core")
    spots = [x, x, x - 1, x - 1, x + 1, x + 1, x + 2, x + 2]
    return jnp.stack(
        [2 * lax.rem(s + size, size) + (1 - core if k % 2 else core) for k, s in enumerate(spots)]
    ).astype(jnp.int32)


def lse_of(parts):
    top = functools.reduce(jnp.maximum, [p[0:1] for p in parts])
    total = sum(jnp.exp(p[0:1] - top) for p in parts)
    return jnp.concatenate([top + jnp.log(total), sum(p[1:2] for p in parts)], axis=0)


def local(
    residual, x_in, bc_in, z_in, dt_raw, dt_bias, decay_rate, d_skip, conv_x_weight, conv_x_bias,
    conv_bc_weight, conv_bc_bias, norm_gain, out_weight, final_gain, lm_weight, targets, doc_lengths,
):
    length, inner = x_in.shape
    heads = dt_raw.shape[0]
    ranks = lax.axis_size(HEADS_AXES)
    seq_size = lax.axis_size("seq")
    groups = lax.axis_size("groups")
    seq_rank = lax.axis_index("seq")
    head_rank = lax.axis_index(HEADS_AXES)
    parity = lax.rem(lax.axis_index("groups"), 2)
    mates = swapped(groups, 1)
    offset = (seq_rank * length).reshape(1).astype(jnp.int32)
    share = residual.shape[1]
    depth = share * ranks

    vocab = lm_weight.shape[1]
    block = 256
    width = -(-vocab // (2 * block)) * block
    overlap = 2 * width - vocab
    first_column = parity * (vocab - width)
    mine = lax.dynamic_slice_in_dim(lm_weight, first_column, width, 1)
    embedding = lax.all_gather(mine, "seq", axis=0, tiled=True)

    onward = [(i, i + 1) for i in range(seq_size - 1)]
    x_rim, bc_rim = lax.ppermute((x_in[length - RIM :], bc_in[length - RIM :]), "seq", onward)
    head_table = jnp.stack([dt_bias, decay_rate], axis=1)
    values, kq, cols, rows, state, through = pl.pallas_call(
        front_kernel,
        out_shape=(
            shape((length, inner), BF16),
            shape((length, 2 * STATE), BF16),
            shape((length, LANES), F32),
            shape((32, length), F32),
            shape((STATE, inner), F32),
            shape((8, inner), F32),
        ),
        in_specs=[SMEM, SMEM] + [pl.BlockSpec()] * 10,
        scratch_shapes=[
            pltpu.VMEM((length + RIM, inner), F32),
            pltpu.VMEM((length + RIM, 2 * STATE), F32),
            pltpu.VMEM((LANES, length), F32),
        ],
        name="front",
    )(
        doc_lengths, offset, x_in, x_rim, bc_in, bc_rim, dt_raw, head_table,
        conv_x_weight, conv_x_bias[None], conv_bc_weight, conv_bc_bias[None],
    )

    incoming = lax.ppermute(state, "seq", onward)
    for _ in range(-(-(LONGEST - 1) // length) - 1):
        incoming = lax.ppermute(state + through[7:8] * incoming, "seq", onward)

    inside = pl.pallas_call(
        intra_kernel,
        out_shape=shape((length, inner), F32),
        in_specs=[SMEM, SMEM] + [pl.BlockSpec()] * 4,
        cost_estimate=cost(16e9, 4e6),
        name="intra",
    )(doc_lengths, offset, kq, values, cols, rows)

    out_weight, _ = lax.optimization_barrier((out_weight, through))
    turned = out_weight.T.reshape(ranks, share, inner)
    weights = lax.all_to_all(turned, HEADS_AXES, 0, 0, tiled=True)

    skip = jnp.repeat(d_skip, HEAD_SIZE)[None]
    gated, squares = pl.pallas_call(
        gate_kernel,
        out_shape=(shape((length, inner), F32), shape((1, length), F32)),
        name="gate",
    )(kq, incoming, cols, inside, values, z_in, skip)
    squares = lax.psum(squares, HEADS_AXES)
    scale = lax.rsqrt(squares[0] / (inner * ranks) + EPSILON)
    normed = (gated * scale[:, None] * norm_gain.astype(F32)[None, :]).astype(BF16)

    order = order_here()
    near, far = around_x(normed, 0)
    partial = pl.pallas_call(
        project_first_kernel,
        out_shape=shape((share, length), F32),
        in_specs=[SMEM] + [pl.BlockSpec()] * 7,
        cost_estimate=cost(6e9, 8e6),
        name="project_first",
    )(order, weights, *near)
    far_a, far_b, far_a_other, far_b_other = far
    block_out = pl.pallas_call(
        project_last_kernel,
        out_shape=shape((share, length), BF16),
        in_specs=[SMEM] + [pl.BlockSpec()] * 7,
        name="project_last",
    )(order, weights, partial, residual.T, far_a, far_b, far_a_other, far_b_other)

    theirs = lax.ppermute(block_out, "groups", mates)
    near, far = around_x(block_out, 1)
    their_near, their_far = around_x(theirs, 1)
    their_targets = lax.ppermute(targets, "groups", mates)
    wanted = jnp.concatenate([targets, their_targets]) - head_rank * vocab
    meta = jnp.stack([parity, first_column]).astype(jnp.int32)
    members = 2
    whole = pl.BlockSpec()
    losses = pl.pallas_call(
        functools.partial(logits_kernel, members=members, overlap=overlap),
        out_shape=shape((2, members * length), F32),
        grid=(width // block,),
        in_specs=[SMEM, SMEM] + [whole] * 22 + [pl.BlockSpec((depth, block), lambda i: (0, i))],
        out_specs=pl.BlockSpec((2, members * length), lambda i: (0, 0)),
        scratch_shapes=[
            pltpu.VMEM((depth, length), BF16),
            pltpu.VMEM((members * length, depth), BF16),
            pltpu.VMEM((members * length, LANES), F32),
            pltpu.VMEM((members * length, LANES), F32),
            pltpu.VMEM((members * length, LANES), F32),
            pltpu.VMEM((members * length, LANES), jnp.int32),
        ],
        name="logits",
    )(
        order, meta, *near, *far, *their_near, *their_far,
        final_gain.astype(F32)[:, None], wanted[:, None], embedding,
    )

    given = lax.ppermute(losses[:, length:], "groups", mates)
    parts = lse_of([losses[:, :length], given])
    parts = lse_of([parts, lax.ppermute(parts, "core", swapped(2, 1))])
    size = lax.axis_size("x")
    parts = lse_of([parts] + [lax.ppermute(parts, "x", ring(size, k)) for k in range(1, size)])
    tokens = (parts[0:1] - parts[1:2])[0]

    ends = jnp.cumsum(doc_lengths)
    positions = offset[0] + jnp.arange(length, dtype=jnp.int32)
    member = (positions[:, None] < ends[None, :]) & (positions[:, None] >= (ends - doc_lengths)[None, :])
    sums = jnp.sum(jnp.where(member, tokens[:, None], 0.0), axis=0)
    everyone = jnp.broadcast_to(sums[None, None], (seq_size, 1, sums.shape[0]))
    sums = lax.all_to_all(everyone, "seq", 0, 0, tiled=True).sum(axis=(0, 1))
    return block_out.T, sums / doc_lengths.astype(F32)


def solution(mesh):
    groups, seq, head = (mesh.shape[name] for name in ("groups", "seq", "head"))
    split = Mesh(mesh.devices.reshape(groups, seq, head // 2, 2), ("groups", "seq", "x", "core"))
    tokens = ("groups", "seq")
    heads = HEADS_AXES
    in_specs = (
        P(tokens, heads), P(tokens, heads), P(tokens, None), P(tokens, heads), P(heads, tokens),
        P(heads), P(heads), P(heads), P(None, heads), P(heads), P(), P(), P(heads), P(heads, None),
        P(), P("seq", heads), P(tokens), P("groups"),
    )
    out_specs = (P(tokens, heads), P("groups"))
    return jax.shard_map(local, mesh=split, in_specs=in_specs, out_specs=out_specs, check_vma=False)
```

time: 458 us -> 282 us (0.62)
  waiting for transfers between devices: 155 us -> 57.5 us
  starting transfers between devices: 19.1 us -> 87.2 us
  blocking collectives: 106 us -> 44.1 us
  local copies, waits for them, and re-layouts: 69.2 us -> 22.6 us
  Pallas kernels: 0 us -> 44.7 us
  matrix products: 40.9 us -> 0 us
  other arithmetic: 44.6 us -> 5.73 us
    all_to_all x2 -> x1, waiting for transfers between devices: 92.6 us -> 0.01 us  [local(): weights = lax.all_to_all(turned, HEADS_AXES, 0, 0, tiled=True)]
    ppermute x2 -> x39, starting transfers between devices: 9.41 us -> 82.1 us  [the longest x2 14.9 us: local(): incoming = lax.ppermute(state + through[7:8] * incoming, 'seq', onward)]
    all_gather x2 -> x1, waiting for transfers between devices: 61.4 us -> 0.02 us  [local(): embedding = lax.all_gather(mine, 'seq', axis=0, tiled=True)]
    ppermute x2 -> x39, waiting for transfers between devices: 0.01 us -> 57.4 us  [the longest x3 14 us: around_x(): left = lax.ppermute(piece, 'x', ring(size, 1))]
    unnamed x1 -> x0, blocking collectives: 44.9 us -> none
    pallas_call x0 -> x6, Pallas kernels: none -> 44.7 us  [the longest x1 20.7 us: local(): pl.pallas_call(functools.partial(logits_kernel, members=members, overlap=...]
    dot_general x12 -> x0, matrix products: 40.9 us -> none  [the longest x1 14.5 us: local(): jnp.dot(hidden, lax.all_gather(lm_weight, 'seq', axis=0, tiled=True), pre...]
    dynamic_update_slice x4 -> x0, local copies, waits for them, and re-layouts: 31.3 us -> none  [local(): lax.scan(advance, jnp.zeros((heads_here, HEAD_SIZE, STATE), jnp.float32),...]
  transfers between devices with their start and end apart: 6 -> 41, of which waited for: 4 -> 16; matrix products, arithmetic and copies ran while one was open for 10% -> 7% of each run, Pallas kernels for 0% -> 9%
where the time goes in v1:
time: 282 us; the launch traced here: 276 us
  starting transfers between devices  87.2 us (31%)
  waiting for transfers between devices  57.5 us (20%)
  Pallas kernels  44.7 us (16%)
  blocking collectives  44.1 us (16%)
  local copies, waits for them, and re-layouts  22.6 us (8%)
  between operations  14.7 us (5%)
  other arithmetic  5.73 us (2%)
    all_to_all x1, blocking collectives, local(): sums = lax.all_to_all(everyone, 'seq', 0, 0, tiled=True).sum(axis=(0, 1))  26.1 us
    pallas_call x1, Pallas kernels, local(): pl.pallas_call(functools.partial(logits_kernel, members=members, overlap=...  20.7 us
    psum x1, blocking collectives, local(): squares = lax.psum(squares, HEADS_AXES)  18 us
    ppermute x2, starting transfers between devices, local(): incoming = lax.ppermute(state + through[7:8] * incoming, 'seq', onward)  14.9 us
    ppermute x3, waiting for transfers between devices, around_x(): left = lax.ppermute(piece, 'x', ring(size, 1))  14 us
    ppermute x1, starting transfers between devices, local(): theirs = lax.ppermute(block_out, 'groups', mates)  11.2 us
    ppermute x3, waiting for transfers between devices, around_x(): lax.ppermute(lax.slice_in_dim(left, 0, half, axis=dim), 'x', ring(size, 1))  11 us
    ppermute x2, waiting for transfers between devices, local(): incoming = lax.ppermute(state + through[7:8] * incoming, 'seq', onward)  10.7 us
  transfers between devices with their start and end apart: 41, of which 16 were waited for; matrix products, arithmetic and copies ran while one was open for 7% of the time, Pallas kernels for 9%

profile of v1, /device:TPU:40, one launch (start us, length us, event | category | flops | bytes accessed | tf_op | source)
XLA Modules:
  0.0 276.5 jit_solution(6293676035301151452)
XLA Ops:
  7.3 1.1 copy-done
  8.4 0.9 constant_dynamic-slice_fusion
  9.3 0.7 slice.76
  10.0 4.7 %collective-permute-start = (bf16[8,640]{1,0:T(8,128)(2,1)S(1)}, bf16[8,640]{1,0:T(8,128)(2,1)S(1)}, u32[]{:S(2)}, u32[]{:S(2)}) collective-permute-start(bf16[8,640]{1,0:T(8,128)(2,1)S(1)} %slice.76), channel_id=1, source_target_pairs={{0,8},{8,16},{16,24},{24,32},{32,40},{40,48},{48,56},{56,64},{64,7... | collective-permute-start | bytes 30728 | tf_op jit(solution)/shard_map/ppermute | solution.py:330
  14.7 0.7 slice.77
  15.4 4.7 %collective-permute-start.1 = (bf16[8,256]{1,0:T(8,128)(2,1)S(1)}, bf16[8,256]{1,0:T(8,128)(2,1)S(1)}, u32[]{:S(2)}, u32[]{:S(2)}) collective-permute-start(bf16[8,256]{1,0:T(8,128)(2,1)S(1)} %slice.77), channel_id=1, source_target_pairs={{0,8},{8,16},{16,24},{24,32},{32,40},{40,48},{48,56},{56,64},{64,7... | collective-permute-start | bytes 12296 | tf_op jit(solution)/shard_map/ppermute | solution.py:330
  20.2 0.7 copy.47.hp_ref
  22.7 4.9 %front.1 = (bf16[512,640]{1,0:T(8,128)(2,1)}, bf16[512,256]{1,0:T(8,128)(2,1)}, f32[512,128]{1,0:T(8,128)}, f32[32,512]{1,0:T(8,128)}, f32[128,640]{1,0:T(8,128)}, /*index=5*/f32[8,640]{1,0:T(8,128)}) custom-call(s32[16]{0:T(128)} %lens.3, s32[1]{0:T(128)} %bitcast.8.offset_ref, bf16[512,640]{1,0:T(8,128)(2,1)} %x_ref.1, bf16[8,640]{1,0:T(8,128)(2,1)} %copy-done.20, ...), custom_call_target="tpu_custom_call" | custom-call | tf_op jit(solution)/shard_map/front/pallas_call | solution.py:332
  27.6 4.7 %collective-permute-start.2 = (f32[128,640]{1,0:T(8,128)}, f32[128,640]{1,0:T(8,128)S(1)}, u32[]{:S(2)}, u32[]{:S(2)}) collective-permute-start(f32[128,640]{1,0:T(8,128)} %get-tuple-element.14), channel_id=1, source_target_pairs={{0,8},{8,16},{16,24},{24,32},{32,40},{40,48},{48,56},{56,64},{64,7... | collective-permute-start | bytes 983048 | tf_op jit(solution)/shard_map/ppermute | solution.py:354
  32.3 0.7 slice_reduce_fusion
  33.0 8.3 %collective-permute-done.2 = f32[128,640]{1,0:T(8,128)S(1)} collective-permute-done((f32[128,640]{1,0:T(8,128)}, f32[128,640]{1,0:T(8,128)S(1)}, u32[]{:S(2)}, u32[]{:S(2)}) %collective-permute-start.2) | collective-permute-done | bytes 327712 | tf_op jit(solution)/shard_map/ppermute | solution.py:354
  41.4 1.0 multiply_add_fusion.1
  42.4 8.9 %collective-permute-start.3 = (f32[128,640]{1,0:T(8,128)S(1)}, f32[128,640]{1,0:T(8,128)S(1)}, u32[]{:S(2)}, u32[]{:S(2)}) collective-permute-start(f32[128,640]{1,0:T(8,128)S(1)} %multiply_add_fusion.1), channel_id=1, source_target_pairs={{0,8},{8,16},{16,24},{24,32},{32,40},{40,48},{48,56},{56,64},{64,7... | collective-permute-start | bytes 983048 | tf_op jit(solution)/shard_map/ppermute | solution.py:356
  51.4 0.7 broadcast_in_dim_reshape.3.skip_ref
  52.0 5.7 %copy.48 = bf16[2560,640]{1,0:T(8,128)(2,1)} copy(bf16[2560,640]{0,1:T(8,128)(2,1)} %bitcast.24) | data formatting | bytes 6553600 | tf_op jit(solution)/shard_map/transpose | solution.py:367
  57.8 5.0 %all-to-all-start = ((bf16[8,320,640]{2,1,0:T(8,128)(2,1)}), bf16[8,320,640]{2,1,0:T(8,128)(2,1)}, u32[]{:S(2)}, u32[]{:S(2)}) async-start(bf16[8,320,640]{2,1,0:T(8,128)(2,1)} %bitcast.23), calls=%async_computation | async-start | bytes 6553600 | tf_op jit(solution)/shard_map/all_to_all | solution.py:368
  62.7 1.7 collective-permute-done.3
  64.5 6.0 %collective-permute-start.4 = (f32[128,640]{1,0:T(8,128)S(1)}, f32[128,640]{1,0:T(8,128)S(1)}, u32[]{:S(2)}, u32[]{:S(2)}) collective-permute-start(f32[128,640]{1,0:T(8,128)S(1)} %multiply_add_fusion), channel_id=1, source_target_pairs={{0,8},{8,16},{16,24},{24,32},{32,40},{40,48},{48,56},{56,64},{64,7... | collective-permute-start | bytes 983048 | tf_op jit(solution)/shard_map/ppermute | solution.py:356
  70.5 5.4 %intra.1.y_ref = f32[512,640]{1,0:T(8,128)} custom-call(s32[16]{0:T(128)} %lens.3, s32[1]{0:T(128)} %bitcast.8.offset_ref, bf16[512,256]{1,0:T(8,128)(2,1)} %get-tuple-element.13.kq_ref, bf16[512,640]{1,0:T(8,128)(2,1)} %get-tuple-element.16.val_ref, f32[512,128]{1,0:T(8,128)} %get-tuple-element.15.cols_ref, f32[32,512]{1,0:T(8,128)} %get-tuple-element.17.rows_ref), custom_call_target="tpu_custom_call" | custom-call | flops 16000000000 | bytes 4000000 | tf_op jit(solution)/shard_map/intra/pallas_call | solution.py:358
  75.9 9.0 %collective-permute-done.4.s_ref = f32[128,640]{1,0:T(8,128)S(1)} collective-permute-done((f32[128,640]{1,0:T(8,128)S(1)}, f32[128,640]{1,0:T(8,128)S(1)}, u32[]{:S(2)}, u32[]{:S(2)}) %collective-permute-start.4) | collective-permute-done | bytes 327712 | tf_op jit(solution)/shard_map/ppermute | solution.py:356
  84.9 0.7 copy-done.11
  85.7 3.9 %gate.1 = (f32[512,640]{1,0:T(8,128)}, f32[1,512]{1,0:T(1,128)}) custom-call(bf16[512,256]{1,0:T(8,128)(2,1)} %get-tuple-element.13.kq_ref, f32[128,640]{1,0:T(8,128)} %copy-done.11, f32[512,128]{1,0:T(8,128)} %get-tuple-element.15.cols_ref, f32[512,640]{1,0:T(8,128)} %intra.1.y_ref, bf16[512,640]{1,0:T(8,128)(2,1)} %get-tuple-element.16.val_ref, ...), custom_call_target="tpu_custom_call" | custom-call | tf_op jit(solution)/shard_map/gate/pallas_call | solution.py:371
  89.6 18.0 %psum.7 = f32[1,512]{1,0:T(1,128)S(1)} all-reduce(f32[1,512]{1,0:T(1,128)} %get-tuple-element.19), channel_id=1, replica_groups=mesh['groups'=2,'seq'=16,'x'=4,'core'=2] {'x','core'}, use_global_device_ids=true, to_apply=%region_0.0 | all-reduce | flops 512 | bytes 4096 | tf_op jit(solution)/shard_map/psum | solution.py:376
  107.6 1.5 multiply_convert_fusion.p0
  109.1 1.6 collective-permute-start.6
  110.7 1.8 collective-permute-start.8
  112.5 14.0 %collective-permute-done.6.p2 = bf16[512,640]{1,0:T(8,128)(2,1)} collective-permute-done((bf16[512,640]{1,0:T(8,128)(2,1)S(1)}, bf16[512,640]{1,0:T(8,128)(2,1)}, u32[]{:S(2)}, u32[]{:S(2)}) %collective-permute-start.6) | collective-permute-done | bytes 655392 | tf_op jit(solution)/shard_map/ppermute | solution.py:276
  127.3 1.0 slice.98
  128.8 1.0 slice.99
  129.8 3.0 %collective-permute-start.11 = (bf16[256,640]{1,0:T(8,128)(2,1)S(1)}, bf16[256,640]{1,0:T(8,128)(2,1)S(1)}, u32[]{:S(2)}, u32[]{:S(2)}) collective-permute-start(bf16[256,640]{1,0:T(8,128)(2,1)S(1)} %slice.99), channel_id=1, source_target_pairs={{0,6},{2,0},{4,2},{6,4},{1,7},{3,1},{5,3},{7,5},{8,14},{10,8},{12,... | collective-permute-start | bytes 983048 | tf_op jit(solution)/shard_map/ppermute | solution.py:280
  133.4 6.0 %collective-permute-done.10.a0 = bf16[256,640]{1,0:T(8,128)(2,1)S(1)} collective-permute-done((bf16[256,640]{1,0:T(8,128)(2,1)S(1)}, bf16[256,640]{1,0:T(8,128)(2,1)S(1)}, u32[]{:S(2)}, u32[]{:S(2)}) %collective-permute-start.10) | collective-permute-done | bytes 327712 | tf_op jit(solution)/shard_map/ppermute | solution.py:279
  139.9 5.7 %project_first.1.acc_ref = f32[320,512]{1,0:T(8,128)} custom-call(s32[8]{0:T(128)} %stack.53.order, bf16[8,320,640]{2,1,0:T(8,128)(2,1)} %all-to-all-done.w_ref, bf16[512,640]{1,0:T(8,128)(2,1)} %copy-done.6, bf16[512,640]{1,0:T(8,128)(2,1)} %collective-permute-done.5.p1, bf16[512,640]{1,0:T(8,128)(2,1)} %collective-permute-done.6.p2, ...), custom_call_target="tpu_custom_call" | custom-call | flops 6000000000 | bytes 8000000 | tf_op jit(solution)/shard_map/project_first/pallas_call | solution.py:382
  145.6 0.7 copy-done.9
  146.4 4.1 %project_last.1.refs_0_ = bf16[320,512]{1,0:T(8,128)(2,1)} custom-call(s32[8]{0:T(128)} %stack.53.order, bf16[8,320,640]{2,1,0:T(8,128)(2,1)} %all-to-all-done.w_ref, f32[320,512]{1,0:T(8,128)} %project_first.1.acc_ref, bf16[320,512]{1,0:T(8,128)(2,1)} %bitcast.26, bf16[256,640]{1,0:T(8,128)(2,1)} %copy-done.7, bf16[256,640]{1,0:T(8,128)(2,1)} %copy-done.8, ...), custom_call_target="tpu_custom_call" | custom-call | tf_op jit(solution)/shard_map/project_last/pallas_call | solution.py:390
  150.5 11.2 %collective-permute-start.23 = (bf16[320,512]{1,0:T(8,128)(2,1)}, bf16[320,512]{1,0:T(8,128)(2,1)S(1)}, u32[]{:S(2)}, u32[]{:S(2)}) collective-permute-start(bf16[320,512]{1,0:T(8,128)(2,1)} %project_last.1.refs_0_), channel_id=1, source_target_pairs={{0,128},{128,0},{1,129},{129,1},{2,130},{130,2},{3,131},{131,3},{4... | collective-permute-start | bytes 983048 | tf_op jit(solution)/shard_map/ppermute | solution.py:397
  161.7 1.4 collective-permute-start.15
  163.1 2.2 collective-permute-start.17
  165.3 4.8 %collective-permute-done.23.refs_10_ = bf16[320,512]{1,0:T(8,128)(2,1)S(1)} collective-permute-done((bf16[320,512]{1,0:T(8,128)(2,1)}, bf16[320,512]{1,0:T(8,128)(2,1)S(1)}, u32[]{:S(2)}, u32[]{:S(2)}) %collective-permute-start.23) | collective-permute-done | bytes 327712 | tf_op jit(solution)/shard_map/ppermute | solution.py:397
  170.2 1.4 collective-permute-start.25
  171.6 2.2 collective-permute-start.27
  174.0 3.3 %collective-permute-start.20 = (bf16[320,256]{1,0:T(8,128)(2,1)S(1)}, bf16[320,256]{1,0:T(8,128)(2,1)}, u32[]{:S(2)}, u32[]{:S(2)}) collective-permute-start(bf16[320,256]{1,0:T(8,128)(2,1)S(1)} %slice.101), channel_id=1, source_target_pairs={{0,6},{2,0},{4,2},{6,4},{1,7},{3,1},{5,3},{7,5},{8,14},{10,8},{12,... | collective-permute-start | bytes 491528 | tf_op jit(solution)/shard_map/ppermute | solution.py:280
  177.3 1.7 collective-permute-start.33
  179.1 1.8 collective-permute-done.33
  180.9 4.1 %collective-permute-done.19.refs_6_ = bf16[320,256]{1,0:T(8,128)(2,1)S(1)} collective-permute-done((bf16[320,256]{1,0:T(8,128)(2,1)S(1)}, bf16[320,256]{1,0:T(8,128)(2,1)S(1)}, u32[]{:S(2)}, u32[]{:S(2)}) %collective-permute-start.19) | collective-permute-done | bytes 163872 | tf_op jit(solution)/shard_map/ppermute | solution.py:279
  185.1 9.1 %collective-permute-start.18 = (bf16[320,512]{1,0:T(8,128)(2,1)S(1)}, bf16[320,512]{1,0:T(8,128)(2,1)}, u32[]{:S(2)}, u32[]{:S(2)}) collective-permute-start(bf16[320,512]{1,0:T(8,128)(2,1)S(1)} %collective-permute-done.17.refs_4_), channel_id=1, source_target_pairs={{0,1},{1,0},{2,3},{3,2},{4,5},{5,4},{6,7},{7,6},{8,9},{9,8},{10,11... | collective-permute-start | bytes 983048 | tf_op jit(solution)/shard_map/ppermute | solution.py:282
  194.7 0.7 slice.102
  195.4 0.7 slice.103
  196.0 0.9 collective-permute-start.29
  197.6 2.4 collective-permute-start.30
  200.5 1.5 reshape.89.refs_20_
  203.1 0.9 collective-permute-done.29.refs_16_
  204.5 0.8 broadcast_subtract_fusion.refs_21_
  206.6 20.7 %logits.1 = f32[2,1024]{1,0:T(2,128)} custom-call(s32[8]{0:T(128)} %stack.53.order, s32[2]{0:T(128)} %pad_add_fusion.1.meta, bf16[320,512]{1,0:T(8,128)(2,1)} %project_last.1.refs_0_, bf16[320,512]{1,0:T(8,128)(2,1)} %copy-done.13, bf16[320,512]{1,0:T(8,128)(2,1)} %copy-done.2, bf16[320,512]{1,0:T(8,128)(2,1)} %copy-done.14, bf16[320,512]{1,0:T(8,128)(2,1)} %copy-done.3, ...), custom_call_target="tpu_custom_call" | custom-call | tf_op jit(solution)/shard_map/logits/pallas_call | solution.py:405
  227.3 0.7 slice.105
  228.0 1.7 collective-permute-start.34
  229.7 2.1 collective-permute-done.34
  231.8 0.8 log_add_fusion.1
  232.8 1.1 collective-permute-done.35
  234.0 1.7 collective-permute-start.36
  235.6 3.3 %collective-permute-start.37 = (f32[2,512]{1,0:T(2,128)S(1)}, f32[2,512]{1,0:T(2,128)S(1)}, u32[]{:S(2)}, u32[]{:S(2)}) collective-permute-start(f32[2,512]{1,0:T(2,128)S(1)} %pad_maximum_fusion.1), channel_id=1, source_target_pairs={{0,4},{2,6},{4,0},{6,2},{1,5},{3,7},{5,1},{7,3},{8,12},{10,14},{12... | collective-permute-start | bytes 12296 | tf_op jit(solution)/shard_map/ppermute | solution.py:429
  238.9 0.9 collective-permute-start.38
  240.1 0.7 collective-permute-done.37
  240.7 1.8 collective-permute-done.38
  242.8 26.1 %all_to_all.10 = f32[16,1,16]{2,1,0:T(1,128)S(1)} all-to-all(f32[16,1,16]{2,1,0:T(1,128)S(1)} %broadcast_in_dim.49), channel_id=1, replica_groups=mesh['groups'=2,'seq'=16,'x'=4,'core'=2] {'seq'}, dimensions={0} | all-to-all | bytes 2048 | tf_op jit(solution)/shard_map/all_to_all | solution.py:437
  (132 shorter events, 10.7 us)
Async XLA Ops:
  7.2 1.2 copy-start
  7.2 13.0 %copy-start.28 = (f32[10]{0:T(128)S(1)}, f32[10]{0:T(128)}, u32[]{:S(2)}) copy-start(f32[10]{0:T(128)} %param.24) | copy-start | bytes 124
  7.2 13.0 %copy-start.29 = (f32[10]{0:T(128)S(1)}, f32[10]{0:T(128)}, u32[]{:S(2)}) copy-start(f32[10]{0:T(128)} %param.23) | copy-start | bytes 124
  7.2 13.7 %copy-start.25 = (bf16[640]{0:T(1024)(128)(2,1)S(1)}, bf16[640]{0:T(1024)(128)(2,1)}, u32[]{:S(2)}) copy-start(bf16[640]{0:T(1024)(128)(2,1)} %param.27) | copy-start | bytes 3844
  7.2 14.2 %copy-start.30 = (bf16[256]{0:T(256)(128)(2,1)S(1)}, bf16[256]{0:T(256)(128)(2,1)}, u32[]{:S(2)}) copy-start(bf16[256]{0:T(256)(128)(2,1)} %param.29) | copy-start | bytes 1540
  7.2 198.7 %all-gather.2.cloned.1.call-start = ((), (), s32[]{:S(2)}) async-start(), calls=%async_computation.2 | async-start | bytes 9748480 | tf_op jit(solution)/shard_map/all_gather | solution.py:327
  9.3 42.0 %copy-start.27 = (f32[10]{0:T(128)S(1)}, f32[10]{0:T(128)}, u32[]{:S(2)}) copy-start(f32[10]{0:T(128)} %param.25) | copy-start | bytes 124
  9.3 42.8 %copy-start.24 = (bf16[640]{0:T(1024)(128)(2,1)S(1)}, bf16[640]{0:T(1024)(128)(2,1)}, u32[]{:S(2)}) copy-start(bf16[640]{0:T(1024)(128)(2,1)} %param.30) | copy-start | bytes 3844
  10.0 12.0 %collective-permute-start = (bf16[8,640]{1,0:T(8,128)(2,1)S(1)}, bf16[8,640]{1,0:T(8,128)(2,1)S(1)}, u32[]{:S(2)}, u32[]{:S(2)}) collective-permute-start(bf16[8,640]{1,0:T(8,128)(2,1)S(1)} %slice.76), channel_id=1, source_target_pairs={{0,8},{8,16},{16,24},{24,32},{32,40},{40,48},{48,56},{56,64},{64,7... | collective-permute-start | bytes 30728 | tf_op jit(solution)/shard_map/ppermute | solution.py:330
  15.4 6.6 %collective-permute-start.1 = (bf16[8,256]{1,0:T(8,128)(2,1)S(1)}, bf16[8,256]{1,0:T(8,128)(2,1)S(1)}, u32[]{:S(2)}, u32[]{:S(2)}) collective-permute-start(bf16[8,256]{1,0:T(8,128)(2,1)S(1)} %slice.77), channel_id=1, source_target_pairs={{0,8},{8,16},{16,24},{24,32},{32,40},{40,48},{48,56},{56,64},{64,7... | collective-permute-start | bytes 12296 | tf_op jit(solution)/shard_map/ppermute | solution.py:330
  27.6 13.8 %collective-permute-start.2 = (f32[128,640]{1,0:T(8,128)}, f32[128,640]{1,0:T(8,128)S(1)}, u32[]{:S(2)}, u32[]{:S(2)}) collective-permute-start(f32[128,640]{1,0:T(8,128)} %get-tuple-element.14), channel_id=1, source_target_pairs={{0,8},{8,16},{16,24},{24,32},{32,40},{40,48},{48,56},{56,64},{64,7... | collective-permute-start | bytes 983048 | tf_op jit(solution)/shard_map/ppermute | solution.py:354
  42.4 22.1 %collective-permute-start.3 = (f32[128,640]{1,0:T(8,128)S(1)}, f32[128,640]{1,0:T(8,128)S(1)}, u32[]{:S(2)}, u32[]{:S(2)}) collective-permute-start(f32[128,640]{1,0:T(8,128)S(1)} %multiply_add_fusion.1), channel_id=1, source_target_pairs={{0,8},{8,16},{16,24},{24,32},{32,40},{40,48},{48,56},{56,64},{64,7... | collective-permute-start | bytes 983048 | tf_op jit(solution)/shard_map/ppermute | solution.py:356
  57.8 6.7 %copy-start.1 = (f32[128,640]{1,0:T(8,128)S(1)}, f32[128,640]{1,0:T(8,128)}, u32[]{:S(2)}) copy-start(f32[128,640]{1,0:T(8,128)} %get-tuple-element.14) | copy-start | bytes 983044
  57.8 82.1 %all-to-all-start = ((bf16[8,320,640]{2,1,0:T(8,128)(2,1)}), bf16[8,320,640]{2,1,0:T(8,128)(2,1)}, u32[]{:S(2)}, u32[]{:S(2)}) async-start(bf16[8,320,640]{2,1,0:T(8,128)(2,1)} %bitcast.23), calls=%async_computation | async-start | bytes 6553600 | tf_op jit(solution)/shard_map/all_to_all | solution.py:368
  64.5 20.4 %collective-permute-start.4 = (f32[128,640]{1,0:T(8,128)S(1)}, f32[128,640]{1,0:T(8,128)S(1)}, u32[]{:S(2)}, u32[]{:S(2)}) collective-permute-start(f32[128,640]{1,0:T(8,128)S(1)} %multiply_add_fusion), channel_id=1, source_target_pairs={{0,8},{8,16},{16,24},{24,32},{32,40},{40,48},{48,56},{56,64},{64,7... | collective-permute-start | bytes 983048 | tf_op jit(solution)/shard_map/ppermute | solution.py:356
  109.1 30.8 %copy-start.6 = (bf16[512,640]{1,0:T(8,128)(2,1)}, bf16[512,640]{1,0:T(8,128)(2,1)S(1)}, u32[]{:S(2)}) copy-start(bf16[512,640]{1,0:T(8,128)(2,1)S(1)} %multiply_convert_fusion.p0) | copy-start | bytes 1966084
  109.1 17.4 %collective-permute-start.6 = (bf16[512,640]{1,0:T(8,128)(2,1)S(1)}, bf16[512,640]{1,0:T(8,128)(2,1)}, u32[]{:S(2)}, u32[]{:S(2)}) collective-permute-start(bf16[512,640]{1,0:T(8,128)(2,1)S(1)} %multiply_convert_fusion.p0), channel_id=1, source_target_pairs={{0,2},{2,4},{4,6},{6,0},{1,3},{3,5},{5,7},{7,1},{8,10},{10,12},{12... | collective-permute-start | bytes 1966088 | tf_op jit(solution)/shard_map/ppermute | solution.py:276
  110.7 16.1 %collective-permute-start.8 = (bf16[512,640]{1,0:T(8,128)(2,1)S(1)}, bf16[512,640]{1,0:T(8,128)(2,1)}, u32[]{:S(2)}, u32[]{:S(2)}) collective-permute-start(bf16[512,640]{1,0:T(8,128)(2,1)S(1)} %multiply_convert_fusion.p0), channel_id=1, source_target_pairs={{0,6},{2,0},{4,2},{6,4},{1,7},{3,1},{5,3},{7,5},{8,14},{10,8},{12,... | collective-permute-start | bytes 1966088 | tf_op jit(solution)/shard_map/ppermute | solution.py:277
  112.5 27.4 %collective-permute-start.5 = (bf16[512,640]{1,0:T(8,128)(2,1)S(1)}, bf16[512,640]{1,0:T(8,128)(2,1)}, u32[]{:S(2)}, u32[]{:S(2)}) collective-permute-start(bf16[512,640]{1,0:T(8,128)(2,1)S(1)} %multiply_convert_fusion.p0), channel_id=1, source_target_pairs={{0,1},{1,0},{2,3},{3,2},{4,5},{5,4},{6,7},{7,6},{8,9},{9,8},{10,11... | collective-permute-start | bytes 1966088 | tf_op jit(solution)/shard_map/ppermute | solution.py:278
  126.5 13.4 %collective-permute-start.7 = (bf16[512,640]{1,0:T(8,128)(2,1)}, bf16[512,640]{1,0:T(8,128)(2,1)}, u32[]{:S(2)}, u32[]{:S(2)}) collective-permute-start(bf16[512,640]{1,0:T(8,128)(2,1)} %collective-permute-done.6.p2), channel_id=1, source_target_pairs={{0,1},{1,0},{2,3},{3,2},{4,5},{5,4},{6,7},{7,6},{8,9},{9,8},{10,11... | collective-permute-start | bytes 1966088 | tf_op jit(solution)/shard_map/ppermute | solution.py:281
  126.8 13.1 %collective-permute-start.9 = (bf16[512,640]{1,0:T(8,128)(2,1)}, bf16[512,640]{1,0:T(8,128)(2,1)}, u32[]{:S(2)}, u32[]{:S(2)}) collective-permute-start(bf16[512,640]{1,0:T(8,128)(2,1)} %collective-permute-done.8.p4), channel_id=1, source_target_pairs={{0,1},{1,0},{2,3},{3,2},{4,5},{5,4},{6,7},{7,6},{8,9},{9,8},{10,11... | collective-permute-start | bytes 1966088 | tf_op jit(solution)/shard_map/ppermute | solution.py:282
  128.3 11.1 %collective-permute-start.10 = (bf16[256,640]{1,0:T(8,128)(2,1)S(1)}, bf16[256,640]{1,0:T(8,128)(2,1)S(1)}, u32[]{:S(2)}, u32[]{:S(2)}) collective-permute-start(bf16[256,640]{1,0:T(8,128)(2,1)S(1)} %slice.98), channel_id=1, source_target_pairs={{0,2},{2,4},{4,6},{6,0},{1,3},{3,5},{5,7},{7,1},{8,10},{10,12},{12... | collective-permute-start | bytes 983048 | tf_op jit(solution)/shard_map/ppermute | solution.py:279
  129.8 10.0 %collective-permute-start.11 = (bf16[256,640]{1,0:T(8,128)(2,1)S(1)}, bf16[256,640]{1,0:T(8,128)(2,1)S(1)}, u32[]{:S(2)}, u32[]{:S(2)}) collective-permute-start(bf16[256,640]{1,0:T(8,128)(2,1)S(1)} %slice.99), channel_id=1, source_target_pairs={{0,6},{2,0},{4,2},{6,4},{1,7},{3,1},{5,3},{7,5},{8,14},{10,8},{12,... | collective-permute-start | bytes 983048 | tf_op jit(solution)/shard_map/ppermute | solution.py:280
  139.4 6.2 %copy-start.7 = (bf16[256,640]{1,0:T(8,128)(2,1)}, bf16[256,640]{1,0:T(8,128)(2,1)S(1)}, u32[]{:S(2)}) copy-start(bf16[256,640]{1,0:T(8,128)(2,1)S(1)} %collective-permute-done.10.a0) | copy-start | bytes 983044
  139.4 6.2 %collective-permute-start.12 = (bf16[256,640]{1,0:T(8,128)(2,1)S(1)}, bf16[256,640]{1,0:T(8,128)(2,1)S(1)}, u32[]{:S(2)}, u32[]{:S(2)}) collective-permute-start(bf16[256,640]{1,0:T(8,128)(2,1)S(1)} %collective-permute-done.10.a0), channel_id=1, source_target_pairs={{0,1},{1,0},{2,3},{3,2},{4,5},{5,4},{6,7},{7,6},{8,9},{9,8},{10,11... | collective-permute-start | bytes 983048 | tf_op jit(solution)/shard_map/ppermute | solution.py:283
  139.8 5.8 %copy-start.8 = (bf16[256,640]{1,0:T(8,128)(2,1)}, bf16[256,640]{1,0:T(8,128)(2,1)S(1)}, u32[]{:S(2)}) copy-start(bf16[256,640]{1,0:T(8,128)(2,1)S(1)} %collective-permute-done.11.b0) | copy-start | bytes 983044
  139.8 5.8 %collective-permute-start.13 = (bf16[256,640]{1,0:T(8,128)(2,1)S(1)}, bf16[256,640]{1,0:T(8,128)(2,1)S(1)}, u32[]{:S(2)}, u32[]{:S(2)}) collective-permute-start(bf16[256,640]{1,0:T(8,128)(2,1)S(1)} %collective-permute-done.11.b0), channel_id=1, source_target_pairs={{0,1},{1,0},{2,3},{3,2},{4,5},{5,4},{6,7},{7,6},{8,9},{9,8},{10,11... | collective-permute-start | bytes 983048 | tf_op jit(solution)/shard_map/ppermute | solution.py:284
  145.6 0.8 copy-start.10
  146.4 30.9 %copy-start.26 = (s32[512]{0:T(512)S(1)}, s32[512]{0:T(512)}, u32[]{:S(2)}) copy-start(s32[512]{0:T(512)} %param.34) | copy-start | bytes 6148
  150.5 50.0 %copy-start.21 = (bf16[2560]{0:T(1024)(128)(2,1)S(1)}, bf16[2560]{0:T(1024)(128)(2,1)}, u32[]{:S(2)}) copy-start(bf16[2560]{0:T(1024)(128)(2,1)} %param.32) | copy-start | bytes 15364
  150.5 19.7 %collective-permute-start.23 = (bf16[320,512]{1,0:T(8,128)(2,1)}, bf16[320,512]{1,0:T(8,128)(2,1)S(1)}, u32[]{:S(2)}, u32[]{:S(2)}) collective-permute-start(bf16[320,512]{1,0:T(8,128)(2,1)} %project_last.1.refs_0_), channel_id=1, source_target_pairs={{0,128},{128,0},{1,129},{129,1},{2,130},{130,2},{3,131},{131,3},{4... | collective-permute-start | bytes 983048 | tf_op jit(solution)/shard_map/ppermute | solution.py:397
  161.7 12.2 %collective-permute-start.15 = (bf16[320,512]{1,0:T(8,128)(2,1)}, bf16[320,512]{1,0:T(8,128)(2,1)S(1)}, u32[]{:S(2)}, u32[]{:S(2)}) collective-permute-start(bf16[320,512]{1,0:T(8,128)(2,1)} %project_last.1.refs_0_), channel_id=1, source_target_pairs={{0,2},{2,4},{4,6},{6,0},{1,3},{3,5},{5,7},{7,1},{8,10},{10,12},{12... | collective-permute-start | bytes 983048 | tf_op jit(solution)/shard_map/ppermute | solution.py:276
  163.1 10.9 %collective-permute-start.17 = (bf16[320,512]{1,0:T(8,128)(2,1)}, bf16[320,512]{1,0:T(8,128)(2,1)S(1)}, u32[]{:S(2)}, u32[]{:S(2)}) collective-permute-start(bf16[320,512]{1,0:T(8,128)(2,1)} %project_last.1.refs_0_), channel_id=1, source_target_pairs={{0,6},{2,0},{4,2},{6,4},{1,7},{3,1},{5,3},{7,5},{8,14},{10,8},{12,... | collective-permute-start | bytes 983048 | tf_op jit(solution)/shard_map/ppermute | solution.py:277
  170.2 31.8 %copy-start.12 = (bf16[320,512]{1,0:T(8,128)(2,1)}, bf16[320,512]{1,0:T(8,128)(2,1)S(1)}, u32[]{:S(2)}) copy-start(bf16[320,512]{1,0:T(8,128)(2,1)S(1)} %collective-permute-done.23.refs_10_) | copy-start | bytes 983044
  170.2 24.0 %collective-permute-start.25 = (bf16[320,512]{1,0:T(8,128)(2,1)S(1)}, bf16[320,512]{1,0:T(8,128)(2,1)S(1)}, u32[]{:S(2)}, u32[]{:S(2)}) collective-permute-start(bf16[320,512]{1,0:T(8,128)(2,1)S(1)} %collective-permute-done.23.refs_10_), channel_id=1, source_target_pairs={{0,2},{2,4},{4,6},{6,0},{1,3},{3,5},{5,7},{7,1},{8,10},{10,12},{12... | collective-permute-start | bytes 983048 | tf_op jit(solution)/shard_map/ppermute | solution.py:276
  171.6 22.9 %collective-permute-start.27 = (bf16[320,512]{1,0:T(8,128)(2,1)S(1)}, bf16[320,512]{1,0:T(8,128)(2,1)S(1)}, u32[]{:S(2)}, u32[]{:S(2)}) collective-permute-start(bf16[320,512]{1,0:T(8,128)(2,1)S(1)} %collective-permute-done.23.refs_10_), channel_id=1, source_target_pairs={{0,6},{2,0},{4,2},{6,4},{1,7},{3,1},{5,3},{7,5},{8,14},{10,8},{12,... | collective-permute-start | bytes 983048 | tf_op jit(solution)/shard_map/ppermute | solution.py:277
  173.8 28.2 %copy-start.2 = (bf16[320,512]{1,0:T(8,128)(2,1)}, bf16[320,512]{1,0:T(8,128)(2,1)S(1)}, u32[]{:S(2)}) copy-start(bf16[320,512]{1,0:T(8,128)(2,1)S(1)} %collective-permute-done.15.refs_2_) | copy-start | bytes 983044
  173.9 11.2 %collective-permute-start.19 = (bf16[320,256]{1,0:T(8,128)(2,1)S(1)}, bf16[320,256]{1,0:T(8,128)(2,1)S(1)}, u32[]{:S(2)}, u32[]{:S(2)}) collective-permute-start(bf16[320,256]{1,0:T(8,128)(2,1)S(1)} %slice.100), channel_id=1, source_target_pairs={{0,2},{2,4},{4,6},{6,0},{1,3},{3,5},{5,7},{7,1},{8,10},{10,12},{12... | collective-permute-start | bytes 491528 | tf_op jit(solution)/shard_map/ppermute | solution.py:279
  174.0 29.1 %copy-start.3 = (bf16[320,512]{1,0:T(8,128)(2,1)}, bf16[320,512]{1,0:T(8,128)(2,1)S(1)}, u32[]{:S(2)}) copy-start(bf16[320,512]{1,0:T(8,128)(2,1)S(1)} %collective-permute-done.17.refs_4_) | copy-start | bytes 983044
  174.0 11.0 %collective-permute-start.20 = (bf16[320,256]{1,0:T(8,128)(2,1)S(1)}, bf16[320,256]{1,0:T(8,128)(2,1)}, u32[]{:S(2)}, u32[]{:S(2)}) collective-permute-start(bf16[320,256]{1,0:T(8,128)(2,1)S(1)} %slice.101), channel_id=1, source_target_pairs={{0,6},{2,0},{4,2},{6,4},{1,7},{3,1},{5,3},{7,5},{8,14},{10,8},{12,... | collective-permute-start | bytes 491528 | tf_op jit(solution)/shard_map/ppermute | solution.py:280
  177.3 3.6 %collective-permute-start.33 = (s32[512]{0:T(512)S(1)}, s32[512]{0:T(512)S(1)}, u32[]{:S(2)}, u32[]{:S(2)}) collective-permute-start(s32[512]{0:T(512)S(1)} %copy-done.26), channel_id=1, source_target_pairs={{0,128},{128,0},{1,129},{129,1},{2,130},{130,2},{3,131},{131,3},{4... | collective-permute-start | bytes 6152 | tf_op jit(solution)/shard_map/ppermute | solution.py:400
  180.9 15.1 %collective-permute-start.14 = (bf16[320,512]{1,0:T(8,128)(2,1)}, bf16[320,512]{1,0:T(8,128)(2,1)S(1)}, u32[]{:S(2)}, u32[]{:S(2)}) collective-permute-start(bf16[320,512]{1,0:T(8,128)(2,1)} %project_last.1.refs_0_), channel_id=1, source_target_pairs={{0,1},{1,0},{2,3},{3,2},{4,5},{5,4},{6,7},{7,6},{8,9},{9,8},{10,11... | collective-permute-start | bytes 983048 | tf_op jit(solution)/shard_map/ppermute | solution.py:278
  185.1 17.8 %copy-start.16 = (bf16[320,256]{1,0:T(8,128)(2,1)}, bf16[320,256]{1,0:T(8,128)(2,1)S(1)}, u32[]{:S(2)}) copy-start(bf16[320,256]{1,0:T(8,128)(2,1)S(1)} %collective-permute-done.19.refs_6_) | copy-start | bytes 491524
  185.1 17.1 %collective-permute-start.16 = (bf16[320,512]{1,0:T(8,128)(2,1)S(1)}, bf16[320,512]{1,0:T(8,128)(2,1)S(1)}, u32[]{:S(2)}, u32[]{:S(2)}) collective-permute-start(bf16[320,512]{1,0:T(8,128)(2,1)S(1)} %collective-permute-done.15.refs_2_), channel_id=1, source_target_pairs={{0,1},{1,0},{2,3},{3,2},{4,5},{5,4},{6,7},{7,6},{8,9},{9,8},{10,11... | collective-permute-start | bytes 983048 | tf_op jit(solution)/shard_map/ppermute | solution.py:281
  185.1 17.6 %collective-permute-start.18 = (bf16[320,512]{1,0:T(8,128)(2,1)S(1)}, bf16[320,512]{1,0:T(8,128)(2,1)}, u32[]{:S(2)}, u32[]{:S(2)}) collective-permute-start(bf16[320,512]{1,0:T(8,128)(2,1)S(1)} %collective-permute-done.17.refs_4_), channel_id=1, source_target_pairs={{0,1},{1,0},{2,3},{3,2},{4,5},{5,4},{6,7},{7,6},{8,9},{9,8},{10,11... | collective-permute-start | bytes 983048 | tf_op jit(solution)/shard_map/ppermute | solution.py:282
  194.1 11.2 %copy-start.4 = (bf16[320,512]{1,0:T(8,128)(2,1)}, bf16[320,512]{1,0:T(8,128)(2,1)S(1)}, u32[]{:S(2)}) copy-start(bf16[320,512]{1,0:T(8,128)(2,1)S(1)} %collective-permute-done.25.refs_12_) | copy-start | bytes 983044
  194.1 2.8 %collective-permute-start.21 = (bf16[320,256]{1,0:T(8,128)(2,1)S(1)}, bf16[320,256]{1,0:T(8,128)(2,1)S(1)}, u32[]{:S(2)}, u32[]{:S(2)}) collective-permute-start(bf16[320,256]{1,0:T(8,128)(2,1)S(1)} %collective-permute-done.19.refs_6_), channel_id=1, source_target_pairs={{0,1},{1,0},{2,3},{3,2},{4,5},{5,4},{6,7},{7,6},{8,9},{9,8},{10,11... | collective-permute-start | bytes 491528 | tf_op jit(solution)/shard_map/ppermute | solution.py:283
  194.5 10.8 %copy-start.5 = (bf16[320,512]{1,0:T(8,128)(2,1)}, bf16[320,512]{1,0:T(8,128)(2,1)S(1)}, u32[]{:S(2)}) copy-start(bf16[320,512]{1,0:T(8,128)(2,1)S(1)} %collective-permute-done.27.refs_14_) | copy-start | bytes 983044
  194.5 7.5 %collective-permute-start.22 = (bf16[320,256]{1,0:T(8,128)(2,1)}, bf16[320,256]{1,0:T(8,128)(2,1)}, u32[]{:S(2)}, u32[]{:S(2)}) collective-permute-start(bf16[320,256]{1,0:T(8,128)(2,1)} %collective-permute-done.20.refs_7_), channel_id=1, source_target_pairs={{0,1},{1,0},{2,3},{3,2},{4,5},{5,4},{6,7},{7,6},{8,9},{9,8},{10,11... | collective-permute-start | bytes 491528 | tf_op jit(solution)/shard_map/ppermute | solution.py:284
  196.0 9.3 %copy-start.13 = (bf16[320,512]{1,0:T(8,128)(2,1)}, bf16[320,512]{1,0:T(8,128)(2,1)S(1)}, u32[]{:S(2)}) copy-start(bf16[320,512]{1,0:T(8,128)(2,1)S(1)} %collective-permute-done.14.refs_1_) | copy-start | bytes 983044
  196.0 8.0 %collective-permute-start.29 = (bf16[320,256]{1,0:T(8,128)(2,1)}, bf16[320,256]{1,0:T(8,128)(2,1)}, u32[]{:S(2)}, u32[]{:S(2)}) collective-permute-start(bf16[320,256]{1,0:T(8,128)(2,1)} %slice.102), channel_id=1, source_target_pairs={{0,2},{2,4},{4,6},{6,0},{1,3},{3,5},{5,7},{7,1},{8,10},{10,12},{12... | collective-permute-start | bytes 491528 | tf_op jit(solution)/shard_map/ppermute | solution.py:279
  197.6 6.5 %collective-permute-start.30 = (bf16[320,256]{1,0:T(8,128)(2,1)}, bf16[320,256]{1,0:T(8,128)(2,1)}, u32[]{:S(2)}, u32[]{:S(2)}) collective-permute-start(bf16[320,256]{1,0:T(8,128)(2,1)} %slice.103), channel_id=1, source_target_pairs={{0,6},{2,0},{4,2},{6,4},{1,7},{3,1},{5,3},{7,5},{8,14},{10,8},{12,... | collective-permute-start | bytes 491528 | tf_op jit(solution)/shard_map/ppermute | solution.py:280
  202.0 3.4 %collective-permute-start.24 = (bf16[320,512]{1,0:T(8,128)(2,1)S(1)}, bf16[320,512]{1,0:T(8,128)(2,1)}, u32[]{:S(2)}, u32[]{:S(2)}) collective-permute-start(bf16[320,512]{1,0:T(8,128)(2,1)S(1)} %collective-permute-done.23.refs_10_), channel_id=1, source_target_pairs={{0,1},{1,0},{2,3},{3,2},{4,5},{5,4},{6,7},{7,6},{8,9},{9,8},{10,11... | collective-permute-start | bytes 983048 | tf_op jit(solution)/shard_map/ppermute | solution.py:278
  202.2 3.7 %collective-permute-start.26 = (bf16[320,512]{1,0:T(8,128)(2,1)S(1)}, bf16[320,512]{1,0:T(8,128)(2,1)S(1)}, u32[]{:S(2)}, u32[]{:S(2)}) collective-permute-start(bf16[320,512]{1,0:T(8,128)(2,1)S(1)} %collective-permute-done.25.refs_12_), channel_id=1, source_target_pairs={{0,1},{1,0},{2,3},{3,2},{4,5},{5,4},{6,7},{7,6},{8,9},{9,8},{10,11... | collective-permute-start | bytes 983048 | tf_op jit(solution)/shard_map/ppermute | solution.py:281
  202.6 3.2 %collective-permute-start.28 = (bf16[320,512]{1,0:T(8,128)(2,1)S(1)}, bf16[320,512]{1,0:T(8,128)(2,1)}, u32[]{:S(2)}, u32[]{:S(2)}) collective-permute-start(bf16[320,512]{1,0:T(8,128)(2,1)S(1)} %collective-permute-done.27.refs_14_), channel_id=1, source_target_pairs={{0,1},{1,0},{2,3},{3,2},{4,5},{5,4},{6,7},{7,6},{8,9},{9,8},{10,11... | collective-permute-start | bytes 983048 | tf_op jit(solution)/shard_map/ppermute | solution.py:282
  204.0 1.6 collective-permute-start.31
  204.1 1.8 collective-permute-start.32
  205.4 34.4 %copy-start.23 = (s32[16]{0:T(128)S(1)}, s32[16]{0:T(128)}, u32[]{:S(2)}) copy-start(s32[16]{0:T(128)} %lens.3) | copy-start | bytes 196
  205.9 0.8 copy-start.15
  228.0 3.8 %collective-permute-start.34 = (f32[2,512]{1,0:T(2,128)S(1)}, f32[2,512]{1,0:T(2,128)S(1)}, u32[]{:S(2)}, u32[]{:S(2)}) collective-permute-start(f32[2,512]{1,0:T(2,128)S(1)} %slice.105), channel_id=1, source_target_pairs={{0,128},{128,0},{1,129},{129,1},{2,130},{130,2},{3,131},{131,3},{4... | collective-permute-start | bytes 12296 | tf_op jit(solution)/shard_map/ppermute | solution.py:425
  232.6 1.3 collective-permute-start.35
  234.0 6.1 %collective-permute-start.36 = (f32[2,512]{1,0:T(2,128)S(1)}, f32[2,512]{1,0:T(2,128)S(1)}, u32[]{:S(2)}, u32[]{:S(2)}) collective-permute-start(f32[2,512]{1,0:T(2,128)S(1)} %pad_maximum_fusion.1), channel_id=1, source_target_pairs={{0,2},{2,4},{4,6},{6,0},{1,3},{3,5},{5,7},{7,1},{8,10},{10,12},{12... | collective-permute-start | bytes 12296 | tf_op jit(solution)/shard_map/ppermute | solution.py:429
  235.6 5.1 %collective-permute-start.37 = (f32[2,512]{1,0:T(2,128)S(1)}, f32[2,512]{1,0:T(2,128)S(1)}, u32[]{:S(2)}, u32[]{:S(2)}) collective-permute-start(f32[2,512]{1,0:T(2,128)S(1)} %pad_maximum_fusion.1), channel_id=1, source_target_pairs={{0,4},{2,6},{4,0},{6,2},{1,5},{3,7},{5,1},{7,3},{8,12},{10,14},{12... | collective-permute-start | bytes 12296 | tf_op jit(solution)/shard_map/ppermute | solution.py:429
  238.9 3.6 %collective-permute-start.38 = (f32[2,512]{1,0:T(2,128)S(1)}, f32[2,512]{1,0:T(2,128)S(1)}, u32[]{:S(2)}, u32[]{:S(2)}) collective-permute-start(f32[2,512]{1,0:T(2,128)S(1)} %pad_maximum_fusion.1), channel_id=1, source_target_pairs={{0,6},{2,0},{4,2},{6,4},{1,7},{3,1},{5,3},{7,5},{8,14},{10,8},{12,... | collective-permute-start | bytes 12296 | tf_op jit(solution)/shard_map/ppermute | solution.py:429
  (8 other events, 5.3 us)
Sparse Core Ops, SparseCore 0:
  9.9 144.3 all-gather.1
